TPU v7x, 512 devices: a whole 4x4x16 slice. The times are simulated.
512 devices in a mesh: blk: 32 (over z_lo, x), col: 16 (over y, z_hi, core).
Axes of the slice: x: 4, y: 4, z: 16 (z_hi: 2, z_lo: 8; z = z_hi * 8 + z_lo), core: 2. Of those that a mesh axis runs over, the one named last changes fastest.
Arguments:
- old_vectors: float32 [1024, 262144], P('col', 'blk'), may hold values from -6 to 6
- merge_matrix: float32 [1024, 1024], P('col', 'blk'), may hold values from -0.1875 to 0.1875
- deflation_order: int32 [1024], P('col'), may hold values from 0 to 63, as said below
- kept_counts: int32 [16], P('col'), may hold values from 1 to 64
Outputs:
- new_vectors: float32 [2, 32, 262144], P(None, None, ('blk', 'col'))
Inputs may be any that keep to these rules, and one draw needn't show every extreme that they name: `deflation_order`: each aligned block of 64 entries holds every number 0 to 63 once.
All inputs are finite; a program needn't handle non-finite values.
Results may differ from a plain program's by a relative error of at most 0.0001.
Values sent between devices are 32-bit elements; how exact they have to be, the bound alone decides.
No kernel may reach another device: no remote copies, remote signals or barrier semaphores. Data moves between devices by JAX's collectives and lax.ppermute only.
A program may use at most 64 MiB of HBM per device.

v0:
```python
import jax
import jax.numpy as jnp
from jax import lax
from jax.sharding import PartitionSpec as P

STEPS = 2


def split_up(value, dim, length):
    dims = value.shape
    pieces = value.reshape(*dims[:dim], length, dims[dim] // length, *dims[dim + 1 :])
    return jnp.moveaxis(pieces, dim, 0)


def sent_and_summed(value, axis, dim):
    pieces = split_up(value, dim, lax.axis_size(axis))
    arrived = lax.all_to_all(pieces, axis, split_axis=0, concat_axis=0, tiled=True)
    return arrived.sum(axis=0)


def shifted(value, axis, by):
    length = lax.axis_size(axis)
    return lax.ppermute(value, axis, [(i, (i + by) % length) for i in range(length)])


def multiply(q_block, u_slab):
    return lax.dot_general(
        u_slab,
        q_block,
        (((0,), (0,)), ((), ())),
        precision=lax.Precision.HIGHEST,
        preferred_element_type=jnp.float32,
    )


def column_sums(partials):
    return sent_and_summed(jnp.stack(partials), "col", 2)


def shards(old_vectors, merge_matrix, deflation_order, kept_counts):
    slab_rows = merge_matrix.shape[0]
    picked = jnp.take(merge_matrix, deflation_order, axis=0)
    live_rows = lax.broadcasted_iota(jnp.int32, (slab_rows, 1), 0) < kept_counts[0]
    merged = jnp.where(live_rows, picked, jnp.float32(0.0))
    u_slab = merged
    partials = [multiply(old_vectors, u_slab)]
    u_slab = shifted(u_slab, "blk", -1)
    partials.append(multiply(old_vectors, u_slab))
    summed = column_sums(partials)
    moving = summed[STEPS - 1 : STEPS]
    moving = shifted(moving, "blk", 1)
    return jnp.concatenate([summed[:1], moving], axis=0)


def solution(mesh):
    return jax.shard_map(
        shards,
        mesh=mesh,
        in_specs=(P("col", "blk"), P("col", "blk"), P("col"), P("col")),
        out_specs=P(None, None, ("blk", "col")),
        check_vma=False,
    )
```

profile of v0, /device:TPU:8, one launch (start us, length us, event | category | flops | bytes accessed | tf_op | source)
XLA Modules:
  0.0 147.1 jit_solution(1734566106254533156)
XLA Ops:
  0.0 0.0 copy-start
  0.8 0.7 compare_select_fusion
  1.5 0.7 compare_and_fusion
  2.1 0.8 copy.6
  2.9 0.6 gather_fusion
  3.5 0.1 select_select_fusion
  3.6 15.4 %collective-permute-start = (f32[64,32]{1,0:T(8,128)S(1)}, f32[64,32]{1,0:T(8,128)S(1)}, u32[]{:S(2)}, u32[]{:S(2)}) collective-permute-start(f32[64,32]{1,0:T(8,128)S(1)} %select_select_fusion), channel_id=1, source_target_pairs={{0,496},{16,0},{32,16},{48,32},{64,48},{80,64},{96,80},{112,96},{1... | collective-permute-start | bytes 24584 | tf_op jit(solution)/shard_map/ppermute | solution.py:23
  19.0 0.0 copy-done
  19.0 1.1 fusion.1
  20.1 0.6 copy.9
  20.8 0.6 copy.7
  21.4 0.0 collective-permute-done
  21.4 1.1 fusion.2
  22.5 0.6 copy.10
  23.1 0.6 copy.8
  23.8 0.3 maximum_bitcast_fusion
  24.0 105.7 %all_to_all.5 = f32[16,2,32,512]{3,2,1,0:T(8,128)} all-to-all(f32[16,2,32,512]{3,2,1,0:T(8,128)S(1)} %maximum_bitcast_fusion), channel_id=1, replica_groups=mesh['blk'=32,'col'=16] {'col'}, dimensions={0} | all-to-all | bytes 4194304 | tf_op jit(solution)/shard_map/all_to_all | solution.py:17
  129.7 1.8 %reduce_sum.9 = f32[2,32,512]{2,1,0:T(8,128)S(1)} reduce(f32[16,2,32,512]{3,2,1,0:T(8,128)} %all_to_all.5, f32[]{:T(128)} %constant.17.clone.1), dimensions={0}, to_apply=%region_0.1 | reduce | flops 491520 | bytes 2228228 | tf_op jit(solution)/shard_map/reduce_sum | solution.py:18
  131.5 1.9 %collective-permute-start.1 = (f32[1,32,512]{2,1,0:T(8,128)S(1)}, f32[1,32,512]{2,1,0:T(8,128)S(1)}, u32[]{:S(2)}, u32[]{:S(2)}) collective-permute-start(f32[1,32,512]{2,1,0:T(8,128)S(1)} %get-tuple-element.6), channel_id=1, source_target_pairs={{0,16},{16,32},{32,48},{48,64},{64,80},{80,96},{96,112},{112,128},... | collective-permute-start | bytes 196616 | tf_op jit(solution)/shard_map/ppermute | solution.py:23
  133.4 12.9 %collective-permute-done.1 = f32[1,32,512]{2,1,0:T(8,128)S(1)} collective-permute-done((f32[1,32,512]{2,1,0:T(8,128)S(1)}, f32[1,32,512]{2,1,0:T(8,128)S(1)}, u32[]{:S(2)}, u32[]{:S(2)}) %collective-permute-start.1) | collective-permute-done | bytes 65568 | tf_op jit(solution)/shard_map/ppermute | solution.py:23
  146.4 0.7 pad_maximum_fusion
  (2 shorter events, 0.0 us)
Async XLA Ops:
  0.0 19.0 %copy-start = (f32[64,8192]{1,0:T(8,128)S(1)}, f32[64,8192]{1,0:T(8,128)}, u32[]{:S(2)}) copy-start(f32[64,8192]{1,0:T(8,128)} %param.4) | copy-start | bytes 6291460
  3.6 17.7 %collective-permute-start = (f32[64,32]{1,0:T(8,128)S(1)}, f32[64,32]{1,0:T(8,128)S(1)}, u32[]{:S(2)}, u32[]{:S(2)}) collective-permute-start(f32[64,32]{1,0:T(8,128)S(1)} %select_select_fusion), channel_id=1, source_target_pairs={{0,496},{16,0},{32,16},{48,32},{64,48},{80,64},{96,80},{112,96},{1... | collective-permute-start | bytes 24584 | tf_op jit(solution)/shard_map/ppermute | solution.py:23
  131.5 14.9 %collective-permute-start.1 = (f32[1,32,512]{2,1,0:T(8,128)S(1)}, f32[1,32,512]{2,1,0:T(8,128)S(1)}, u32[]{:S(2)}, u32[]{:S(2)}) collective-permute-start(f32[1,32,512]{2,1,0:T(8,128)S(1)} %get-tuple-element.6), channel_id=1, source_target_pairs={{0,16},{16,32},{32,48},{48,64},{64,80},{80,96},{96,112},{112,128},... | collective-permute-start | bytes 196616 | tf_op jit(solution)/shard_map/ppermute | solution.py:23
where the time goes:
time: 147 us
  blocking collectives  106 us (72%)
  starting transfers between devices  17.3 us (12%)
  waiting for transfers between devices  12.9 us (9%)
  other arithmetic  4.1 us (3%)
  local copies, waits for them, and re-layouts  3.86 us (3%)
  matrix products  2.26 us (2%)
    all_to_all x1, blocking collectives, sent_and_summed(): lax.all_to_all(pieces, axis, split_axis=0, concat_axis=0, tiled=True)  106 us
    ppermute x2, starting transfers between devices, shifted(): lax.ppermute(value, axis, [(i, (i + by) % length) for i in range(length)])  17.3 us
    ppermute x2, waiting for transfers between devices, shifted(): lax.ppermute(value, axis, [(i, (i + by) % length) for i in range(length)])  12.9 us
  transfers between devices with their start and end apart: 2, of which 1 were waited for; matrix products, arithmetic and copies ran while one was open for 2% of the time, Pallas kernels for 0%

commit v1 on v0

v1 whole, which is shorter than its diff:
```python
import functools

import jax
import jax.numpy as jnp
from jax import lax
from jax.experimental import pallas as pl
from jax.experimental.pallas import tpu as pltpu
from jax.sharding import Mesh, PartitionSpec as P

AXES = ("zl", "x", "y", "zh", "core")
SIZES = (8, 4, 4, 2, 2)
NBLK = 32


def prep_kernel(core_ref, kept_ref, order_ref, merge_ref, q_ref, ut_ref, send_ref, sem):
    other = 1 - core_ref[0]
    pieces = send_ref.shape[0]
    width = send_ref.shape[2]
    copies = []
    for g in range(pieces):
        start = pl.multiple_of((2 * g + other) * width, width)
        copies.append(pltpu.make_async_copy(q_ref.at[:, pl.ds(start, width)], send_ref.at[g], sem.at[g]))
    for c in copies:
        c.start()
    n = merge_ref.shape[0]
    rows = lax.broadcasted_iota(jnp.int32, (n, n), 0)
    place = lax.broadcasted_iota(jnp.int32, (n, n), 1)
    hit = (rows == order_ref[...]) & (place < kept_ref[0])
    ut_ref[...] = lax.dot_general(
        merge_ref[...],
        hit.astype(jnp.float32),
        (((0,), (0,)), ((), ())),
        precision=lax.Precision.HIGHEST,
        preferred_element_type=jnp.float32,
    )
    for c in copies:
        c.wait()


def prepare(core, kept, order, merge, q):
    k, j = merge.shape
    pieces, width = 8, q.shape[1] // 16
    return pl.pallas_call(
        prep_kernel,
        out_shape=(
            jax.ShapeDtypeStruct((j, k), jnp.float32),
            jax.ShapeDtypeStruct((pieces, k, width), jnp.float32),
        ),
        in_specs=[
            pl.BlockSpec(memory_space=pltpu.SMEM),
            pl.BlockSpec(memory_space=pltpu.SMEM),
            pl.BlockSpec(memory_space=pltpu.VMEM),
            pl.BlockSpec(memory_space=pltpu.VMEM),
            pl.BlockSpec(memory_space=pl.ANY),
        ],
        out_specs=(
            pl.BlockSpec(memory_space=pltpu.VMEM),
            pl.BlockSpec(memory_space=pl.ANY),
        ),
        scratch_shapes=[pltpu.SemaphoreType.DMA((pieces,))],
        name="prep",
    )(core, kept, order, merge, q)


def multiply_kernel(where_ref, ut_ref, q_ref, got_ref, out_ref):
    core, zh, flip = where_ref[0], where_ref[1], where_ref[2]
    g = pl.program_id(0)
    zt = g % 2
    j = ut_ref.shape[1] // 2
    u = jnp.concatenate([ut_ref[core], ut_ref[1 - core]], axis=1)
    qq = jnp.concatenate([q_ref[...], got_ref[0]], axis=0)
    prod = lax.dot_general(
        u,
        qq,
        (((1,), (0,)), ((), ())),
        precision=lax.Precision.HIGHEST,
        preferred_element_type=jnp.float32,
    )
    late0 = (zt == zh).astype(jnp.int32)
    late1 = (late0 + flip) % 2
    out_ref[late0, g // 2, 0:j, :] = prod[0:j]
    out_ref[late1, g // 2, j : 2 * j, :] = prod[j : 2 * j]


def multiply(where, ut, q, got):
    pieces, k, width = got.shape
    rows = ut.shape[1]
    return pl.pallas_call(
        multiply_kernel,
        grid_spec=pltpu.PrefetchScalarGridSpec(
            num_scalar_prefetch=1,
            grid=(pieces,),
            in_specs=[
                pl.BlockSpec(ut.shape, lambda g, w: (0, 0, 0)),
                pl.BlockSpec((k, width), lambda g, w: (0, 2 * g + w[0])),
                pl.BlockSpec((1, k, width), lambda g, w: (g, 0, 0)),
            ],
            out_specs=pl.BlockSpec((2, pieces // 2, rows, width), lambda g, w: (0, 0, 0, 0)),
        ),
        out_shape=jax.ShapeDtypeStruct((2, pieces // 2, rows, width), jnp.float32),
        name="multiply",
    )(where, ut, q, got)


def pairs_of(move):
    pairs = []
    for b in range(NBLK):
        for zh in range(2):
            tb, tz = move(b, zh)
            pairs.append((b * 2 + zh, tb * 2 + tz))
    return pairs


BACK = pairs_of(lambda b, zh: ((b - 1) % NBLK, zh))
AHEAD = pairs_of(lambda b, zh: ((b + 1) % NBLK, zh if b < NBLK - 1 else 1 - zh))
SWAP = [(0, 1), (1, 0)]
ROUND = ("zl", "x", "zh")


def shards(old_vectors, merge_matrix, deflation_order, kept_counts):
    core = lax.axis_index("core").astype(jnp.int32)
    zh = lax.axis_index("zh").astype(jnp.int32)
    last = (lax.axis_index(("zl", "x")) == NBLK - 1).astype(jnp.int32)
    k, j = merge_matrix.shape
    ut, send = prepare(core.reshape(1), kept_counts, deflation_order.reshape(1, k), merge_matrix, old_vectors)
    ut_next = lax.ppermute(ut, ROUND, BACK)
    got = lax.ppermute(send, "core", SWAP)
    both = lax.all_gather(jnp.concatenate([ut, ut_next], axis=0), "core")
    parts = multiply(jnp.stack([core, zh, last]), both, old_vectors, got)
    early = lax.all_to_all(parts[0], "y", 0, 0, tiled=True).sum(axis=0)
    early1 = lax.ppermute(early[j:], ROUND, AHEAD)
    across = lax.ppermute(jnp.stack([early[:j], early1]), "zh", SWAP)
    late = lax.all_to_all(parts[1], "y", 0, 0, tiled=True).sum(axis=0)
    late1 = lax.ppermute(late[j:], ROUND, AHEAD)
    return jnp.stack([late[:j], late1]) + across


def solution(mesh):
    split = Mesh(mesh.devices.reshape(SIZES), AXES)
    blk, col = ("zl", "x"), ("y", "zh", "core")
    return jax.shard_map(
        shards,
        mesh=split,
        in_specs=(P(col, blk), P(col, blk), P(col), P(col)),
        out_specs=P(None, None, AXES),
        check_vma=False,
    )
```

time: 147 us -> 128 us (0.87)
  blocking collectives: 106 us -> 15 us
  Pallas kernels: 0 us -> 41.6 us
  waiting for transfers between devices: 12.9 us -> 35.3 us
  starting transfers between devices: 17.3 us -> 27.9 us
  matrix products: 2.26 us -> 0 us
  other arithmetic: 4.1 us -> 2.13 us
    all_to_all x1, blocking collectives: 106 us -> 13 us  [shards(): early = lax.all_to_all(parts[0], 'y', 0, 0, tiled=True).sum(axis=0)]
    pallas_call x0 -> x2, Pallas kernels: none -> 41.6 us  [the longest x1 34.3 us: prepare(): pl.pallas_call(prep_kernel, out_shape=(jax.ShapeDtypeStruct((j, k), jnp.f...]
    ppermute x2 -> x5, waiting for transfers between devices: 12.9 us -> 30.1 us  [the longest x1 17.4 us: shards(): early1 = lax.ppermute(early[j:], ROUND, AHEAD)]
    ppermute x2 -> x5, starting transfers between devices: 17.3 us -> 23 us  [the longest x1 15.4 us: shards(): ut_next = lax.ppermute(ut, ROUND, BACK)]
    all_to_all x0 -> x1, waiting for transfers between devices: none -> 5.21 us  [shards(): late = lax.all_to_all(parts[1], 'y', 0, 0, tiled=True).sum(axis=0)]
    all_to_all x0 -> x1, starting transfers between devices: none -> 4.9 us  [shards(): late = lax.all_to_all(parts[1], 'y', 0, 0, tiled=True).sum(axis=0)]
    dot_general x2 -> x0, matrix products: 2.26 us -> none  [multiply(): lax.dot_general(u_slab, q_block, (((0,), (0,)), ((), ())), precision=lax....]
    squeeze x0 -> x1, local copies, waits for them, and re-layouts: none -> 2.07 us  [shards(): late = lax.all_to_all(parts[1], 'y', 0, 0, tiled=True).sum(axis=0)]
  transfers between devices with their start and end apart: 2 -> 6, of which waited for: 1 -> 5; matrix products, arithmetic and copies ran while one was open for 2% -> 1% of each run, Pallas kernels for 0% -> 0%
where the time goes in v1:
time: 128 us; the launch traced here: 127 us
  Pallas kernels  41.6 us (32%)
  waiting for transfers between devices  35.3 us (28%)
  starting transfers between devices  27.9 us (22%)
  blocking collectives  15 us (12%)
  local copies, waits for them, and re-layouts  4.54 us (4%)
  other arithmetic  2.13 us (2%)
    pallas_call x1, Pallas kernels, prepare(): pl.pallas_call(prep_kernel, out_shape=(jax.ShapeDtypeStruct((j, k), jnp.f...  34.3 us
    ppermute x1, waiting for transfers between devices, shards(): early1 = lax.ppermute(early[j:], ROUND, AHEAD)  17.4 us
    ppermute x1, starting transfers between devices, shards(): ut_next = lax.ppermute(ut, ROUND, BACK)  15.4 us
    all_to_all x1, blocking collectives, shards(): early = lax.all_to_all(parts[0], 'y', 0, 0, tiled=True).sum(axis=0)  13 us
    ppermute x1, waiting for transfers between devices, shards(): late1 = lax.ppermute(late[j:], ROUND, AHEAD)  7.55 us
    pallas_call x1, Pallas kernels, multiply(): pl.pallas_call(multiply_kernel, grid_spec=pltpu.PrefetchScalarGridSpec(nu...  7.28 us
    all_to_all x1, waiting for transfers between devices, shards(): late = lax.all_to_all(parts[1], 'y', 0, 0, tiled=True).sum(axis=0)  5.21 us
    all_to_all x1, starting transfers between devices, shards(): late = lax.all_to_all(parts[1], 'y', 0, 0, tiled=True).sum(axis=0)  4.9 us
  transfers between devices with their start and end apart: 6, of which 5 were waited for; matrix products, arithmetic and copies ran while one was open for 1% of the time, Pallas kernels for 0%

profile of v1, /device:TPU:8, one launch (start us, length us, event | category | flops | bytes accessed | tf_op | source)
XLA Modules:
  0.0 127.3 jit_solution(5522242379087613635)
XLA Ops:
  0.7 1.4 %copy.5.merge_ref = f32[64,32]{1,0:T(8,128)} copy(f32[64,32]{0,1:T(8,128)} %param.5) | data formatting | bytes 16384 | tf_op args[1]
  2.1 34.3 %prep.1 = (f32[32,64]{1,0:T(8,128)}, f32[8,64,512]{2,1,0:T(8,128)}) custom-call(s32[1]{0:T(128)} %bitcast.core_ref, s32[1]{0:T(128)S(6)} %copy.6.kept_ref, s32[1,64]{1,0:T(1,128)} %bitcast.18, f32[64,32]{1,0:T(8,128)} %copy.5.merge_ref, f32[64,8192]{1,0:T(8,128)} %q_ref.3), custom_call_target="tpu_custom_call" | custom-call | tf_op jit(solution)/shard_map/prep/pallas_call | solution.py:43
  36.4 1.9 %collective-permute-start.1 = (f32[8,64,512]{2,1,0:T(8,128)}, f32[8,64,512]{2,1,0:T(8,128)S(1)}, u32[]{:S(2)}, u32[]{:S(2)}) collective-permute-start(f32[8,64,512]{2,1,0:T(8,128)} %get-tuple-element.8), channel_id=1, source_target_pairs={{0,1},{1,0},{2,3},{3,2},{4,5},{5,4},{6,7},{7,6},{8,9},{9,8},{10,11... | collective-permute-start | bytes 3145736 | tf_op jit(solution)/shard_map/ppermute | solution.py:127
  38.3 15.4 %collective-permute-start = (f32[32,64]{1,0:T(8,128)}, f32[32,64]{1,0:T(8,128)S(1)}, u32[]{:S(2)}, u32[]{:S(2)}) collective-permute-start(f32[32,64]{1,0:T(8,128)} %get-tuple-element.7), channel_id=1, source_target_pairs={{0,496},{2,498},{16,0},{18,2},{32,16},{34,18},{48,32},{50,34},{64,... | collective-permute-start | bytes 24584 | tf_op jit(solution)/shard_map/ppermute | solution.py:126
  53.7 0.7 pad_add_fusion.where_ref
  54.3 1.0 collective-permute-done
  55.3 0.7 pad_maximum_fusion.1
  56.0 2.0 %all-gather = f32[128,64]{1,0:T(8,128)} all-gather(f32[64,64]{1,0:T(8,128)S(1)} %pad_maximum_fusion.1), channel_id=2, replica_groups=mesh['zl'=8,'x'=4,'y'=4,'zh'=2,'core'=2] {'core'}, dimensions={0}, use_global_device_ids=true | all-gather | bytes 49152 | tf_op jit(solution)/shard_map/all_gather | solution.py:128
  58.0 0.0 collective-permute-done.1.got_ref
  58.0 0.0 copy-start
  58.0 1.0 copy-done
  59.0 7.3 %multiply.1 = f32[2,4,64,512]{3,2,1,0:T(8,128)} custom-call(s32[3]{0:T(128)} %pad_add_fusion.where_ref, f32[2,64,64]{2,1,0:T(8,128)} %bitcast.15, f32[64,8192]{1,0:T(8,128)} %q_ref.3, f32[8,64,512]{2,1,0:T(8,128)} %copy-done), custom_call_target="tpu_custom_call" | custom-call | tf_op jit(solution)/shard_map/multiply/pallas_call | solution.py:88
  66.3 2.1 %slice_bitcast_fusion.1 = (f32[4,64,512]{2,1,0:T(8,128)}, f32[4,64,512]{2,1,0:T(8,128)S(1)}) fusion(f32[2,4,64,512]{3,2,1,0:T(8,128)} %multiply.1), kind=kLoop, calls=%fused_computation.1 | loop fusion | bytes 2097152 | tf_op jit(solution)/shard_map/squeeze | solution.py:133
  68.4 13.0 %all_to_all.10 = f32[4,64,512]{2,1,0:T(8,128)S(1)} all-to-all(f32[4,64,512]{2,1,0:T(8,128)S(1)} %get-tuple-element.10), channel_id=1, replica_groups=mesh['zl'=8,'x'=4,'y'=4,'zh'=2,'core'=2] {'y'}, dimensions={0} | all-to-all | bytes 1048576 | tf_op jit(solution)/shard_map/all_to_all | solution.py:130
  81.4 4.9 %all-to-all-start = ((f32[4,64,512]{2,1,0:T(8,128)}), f32[4,64,512]{2,1,0:T(8,128)S(1)}, u32[]{:S(2)}, u32[]{:S(2)}) async-start(f32[4,64,512]{2,1,0:T(8,128)} %get-tuple-element.9), calls=%async_computation | async-start | bytes 1048576 | tf_op jit(solution)/shard_map/all_to_all | solution.py:133
  86.4 1.9 %collective-permute-start.3 = (f32[32,512]{1,0:T(8,128)S(1)}, f32[32,512]{1,0:T(8,128)S(1)}, u32[]{:S(2)}, u32[]{:S(2)}) collective-permute-start(f32[32,512]{1,0:T(8,128)S(1)} %get-tuple-element.14), channel_id=1, source_target_pairs={{0,16},{2,18},{16,32},{18,34},{32,48},{34,50},{48,64},{50,66},{64,... | collective-permute-start | bytes 196616 | tf_op jit(solution)/shard_map/ppermute | solution.py:131
  88.3 5.2 %all-to-all-done = f32[4,64,512]{2,1,0:T(8,128)S(1)} async-done(((f32[4,64,512]{2,1,0:T(8,128)}), f32[4,64,512]{2,1,0:T(8,128)S(1)}, u32[]{:S(2)}, u32[]{:S(2)}) %all-to-all-start) | async-done | bytes 524320 | tf_op jit(solution)/shard_map/all_to_all | solution.py:133
  93.6 17.4 %collective-permute-done.3 = f32[32,512]{1,0:T(8,128)S(1)} collective-permute-done((f32[32,512]{1,0:T(8,128)S(1)}, f32[32,512]{1,0:T(8,128)S(1)}, u32[]{:S(2)}, u32[]{:S(2)}) %collective-permute-start.3) | collective-permute-done | bytes 65568 | tf_op jit(solution)/shard_map/ppermute | solution.py:131
  111.0 1.9 %collective-permute-start.4 = (f32[2,32,512]{2,1,0:T(8,128)S(1)}, f32[2,32,512]{2,1,0:T(8,128)S(1)}, u32[]{:S(2)}, u32[]{:S(2)}) collective-permute-start(f32[2,32,512]{2,1,0:T(8,128)S(1)} %pad_maximum_fusion), channel_id=1, source_target_pairs={{0,2},{2,0},{1,3},{3,1},{4,6},{6,4},{5,7},{7,5},{8,10},{10,8},{9,1... | collective-permute-start | bytes 393224 | tf_op jit(solution)/shard_map/ppermute | solution.py:132
  113.0 1.9 %collective-permute-start.2 = (f32[32,512]{1,0:T(8,128)S(1)}, f32[32,512]{1,0:T(8,128)S(1)}, u32[]{:S(2)}, u32[]{:S(2)}) collective-permute-start(f32[32,512]{1,0:T(8,128)S(1)} %get-tuple-element.12), channel_id=1, source_target_pairs={{0,16},{2,18},{16,32},{18,34},{32,48},{34,50},{48,64},{50,66},{64,... | collective-permute-start | bytes 196616 | tf_op jit(solution)/shard_map/ppermute | solution.py:134
  114.9 7.6 %collective-permute-done.2 = f32[32,512]{1,0:T(8,128)S(1)} collective-permute-done((f32[32,512]{1,0:T(8,128)S(1)}, f32[32,512]{1,0:T(8,128)S(1)}, u32[]{:S(2)}, u32[]{:S(2)}) %collective-permute-start.2) | collective-permute-done | bytes 65568 | tf_op jit(solution)/shard_map/ppermute | solution.py:134
  122.5 4.1 %collective-permute-done.4 = f32[2,32,512]{2,1,0:T(8,128)S(1)} collective-permute-done((f32[2,32,512]{2,1,0:T(8,128)S(1)}, f32[2,32,512]{2,1,0:T(8,128)S(1)}, u32[]{:S(2)}, u32[]{:S(2)}) %collective-permute-start.4) | collective-permute-done | bytes 131104 | tf_op jit(solution)/shard_map/ppermute | solution.py:132
  126.6 0.7 maximum_add_fusion
  (5 shorter events, 0.1 us)
Async XLA Ops:
  36.4 21.6 %collective-permute-start.1 = (f32[8,64,512]{2,1,0:T(8,128)}, f32[8,64,512]{2,1,0:T(8,128)S(1)}, u32[]{:S(2)}, u32[]{:S(2)}) collective-permute-start(f32[8,64,512]{2,1,0:T(8,128)} %get-tuple-element.8), channel_id=1, source_target_pairs={{0,1},{1,0},{2,3},{3,2},{4,5},{5,4},{6,7},{7,6},{8,9},{9,8},{10,11... | collective-permute-start | bytes 3145736 | tf_op jit(solution)/shard_map/ppermute | solution.py:127
  38.3 17.0 %collective-permute-start = (f32[32,64]{1,0:T(8,128)}, f32[32,64]{1,0:T(8,128)S(1)}, u32[]{:S(2)}, u32[]{:S(2)}) collective-permute-start(f32[32,64]{1,0:T(8,128)} %get-tuple-element.7), channel_id=1, source_target_pairs={{0,496},{2,498},{16,0},{18,2},{32,16},{34,18},{48,32},{50,34},{64,... | collective-permute-start | bytes 24584 | tf_op jit(solution)/shard_map/ppermute | solution.py:126
  58.0 1.0 copy-start
  81.4 12.1 %all-to-all-start = ((f32[4,64,512]{2,1,0:T(8,128)}), f32[4,64,512]{2,1,0:T(8,128)S(1)}, u32[]{:S(2)}, u32[]{:S(2)}) async-start(f32[4,64,512]{2,1,0:T(8,128)} %get-tuple-element.9), calls=%async_computation | async-start | bytes 1048576 | tf_op jit(solution)/shard_map/all_to_all | solution.py:133
  86.4 24.6 %collective-permute-start.3 = (f32[32,512]{1,0:T(8,128)S(1)}, f32[32,512]{1,0:T(8,128)S(1)}, u32[]{:S(2)}, u32[]{:S(2)}) collective-permute-start(f32[32,512]{1,0:T(8,128)S(1)} %get-tuple-element.14), channel_id=1, source_target_pairs={{0,16},{2,18},{16,32},{18,34},{32,48},{34,50},{48,64},{50,66},{64,... | collective-permute-start | bytes 196616 | tf_op jit(solution)/shard_map/ppermute | solution.py:131
  111.0 15.6 %collective-permute-start.4 = (f32[2,32,512]{2,1,0:T(8,128)S(1)}, f32[2,32,512]{2,1,0:T(8,128)S(1)}, u32[]{:S(2)}, u32[]{:S(2)}) collective-permute-start(f32[2,32,512]{2,1,0:T(8,128)S(1)} %pad_maximum_fusion), channel_id=1, source_target_pairs={{0,2},{2,0},{1,3},{3,1},{4,6},{6,4},{5,7},{7,5},{8,10},{10,8},{9,1... | collective-permute-start | bytes 393224 | tf_op jit(solution)/shard_map/ppermute | solution.py:132
  113.0 9.5 %collective-permute-start.2 = (f32[32,512]{1,0:T(8,128)S(1)}, f32[32,512]{1,0:T(8,128)S(1)}, u32[]{:S(2)}, u32[]{:S(2)}) collective-permute-start(f32[32,512]{1,0:T(8,128)S(1)} %get-tuple-element.12), channel_id=1, source_target_pairs={{0,16},{2,18},{16,32},{18,34},{32,48},{34,50},{48,64},{50,66},{64,... | collective-permute-start | bytes 196616 | tf_op jit(solution)/shard_map/ppermute | solution.py:134

commit v2 on v0

v2 whole, which is shorter than its diff:
```python
import jax
import jax.numpy as jnp
from jax import lax
from jax.experimental import pallas as pl
from jax.experimental.pallas import tpu as pltpu
from jax.sharding import Mesh, PartitionSpec as P

AXES = ("zl", "x", "y", "zh", "core")
SIZES = (8, 4, 4, 2, 2)
NBLK = 32
LIMIT = pltpu.CompilerParams(vmem_limit_bytes=8 * 1024 * 1024)
SMEM = pl.BlockSpec(memory_space=pltpu.SMEM)
VMEM = pl.BlockSpec(memory_space=pltpu.VMEM)
ANY = pl.BlockSpec(memory_space=pl.ANY)


def on_chip(value):
    return pltpu.with_memory_space_constraint(value, pltpu.VMEM)


def dot(a, b, contract):
    return lax.dot_general(
        a, b, (contract, ((), ())), precision=lax.Precision.HIGHEST, preferred_element_type=jnp.float32
    )


def deflate_kernel(kept_ref, order_ref, merge_ref, ut_ref):
    n = merge_ref.shape[1]
    rows = lax.broadcasted_iota(jnp.int32, (n, n), 0)
    place = lax.broadcasted_iota(jnp.int32, (n, n), 1)
    hit = (rows == order_ref[...]) & (place < kept_ref[0])
    ut_ref[...] = dot(merge_ref[...], hit.astype(jnp.float32), ((1,), (0,)))


def deflate(kept, order, merge_t):
    return pl.pallas_call(
        deflate_kernel,
        out_shape=pltpu.VMEM(merge_t.shape, jnp.float32),
        in_specs=[SMEM, VMEM, VMEM],
        out_specs=VMEM,
        compiler_params=LIMIT,
        name="deflate",
    )(kept, order, merge_t)


def divide_kernel(core_ref, q_ref, send_ref, keep_ref, sem):
    pieces, _, width = send_ref.shape
    copies = []
    for side, target in ((1 - core_ref[0], send_ref), (core_ref[0], keep_ref)):
        for g in range(pieces):
            start = pl.multiple_of((2 * g + side) * width, width)
            copies.append(
                pltpu.make_async_copy(q_ref.at[:, pl.ds(start, width)], target.at[g], sem.at[len(copies)])
            )
    for c in copies:
        c.start()
    for c in copies:
        c.wait()


def divide(core, q, pieces):
    half = pltpu.VMEM((pieces, q.shape[0], q.shape[1] // (2 * pieces)), jnp.float32)
    return pl.pallas_call(
        divide_kernel,
        out_shape=(half, half),
        in_specs=[SMEM, ANY],
        out_specs=(VMEM, VMEM),
        scratch_shapes=[pltpu.SemaphoreType.DMA((2 * pieces,))],
        compiler_params=LIMIT,
        name="divide",
    )(core, q)


def multiply_kernel(where_ref, ut_ref, next_ref, keep_ref, got_ref, early_ref, late_ref):
    core, zh, flip = where_ref[0], where_ref[1], where_ref[2]
    j = ut_ref.shape[1]
    mine = jnp.concatenate([ut_ref[core], next_ref[core]], axis=0)
    theirs = jnp.concatenate([ut_ref[1 - core], next_ref[1 - core]], axis=0)
    u = jnp.concatenate([mine, theirs], axis=1)

    def block(g):
        return dot(u, jnp.concatenate([keep_ref[g], got_ref[g]], axis=0), ((1,), (0,)))

    for y in range(early_ref.shape[0]):
        first, second = block(2 * y + 1 - zh), block(2 * y + zh)
        early_ref[y, :j] = first[:j]
        late_ref[y, :j] = second[:j]
        early_ref[y, j:] = jnp.where(flip == 1, second[j:], first[j:])
        late_ref[y, j:] = jnp.where(flip == 1, first[j:], second[j:])


def multiply(where, ut, ut_next, keep, got):
    pieces, _, width = keep.shape
    out = pltpu.VMEM((pieces // 2, 2 * ut.shape[1], width), jnp.float32)
    return pl.pallas_call(
        multiply_kernel,
        out_shape=(out, out),
        in_specs=[SMEM, VMEM, VMEM, VMEM, VMEM],
        out_specs=(VMEM, VMEM),
        compiler_params=LIMIT,
        name="multiply",
    )(where, ut, ut_next, keep, got)


def pairs_of(move):
    pairs = []
    for b in range(NBLK):
        for zh in range(2):
            tb, tz = move(b, zh)
            pairs.append((b * 2 + zh, tb * 2 + tz))
    return pairs


BACK = pairs_of(lambda b, zh: ((b - 1) % NBLK, zh))
AHEAD = pairs_of(lambda b, zh: ((b + 1) % NBLK, zh if b < NBLK - 1 else 1 - zh))
SWAP = [(0, 1), (1, 0)]
ROUND = ("zl", "x", "zh")


def shards(old_vectors, merge_matrix, deflation_order, kept_counts):
    core = lax.axis_index("core").astype(jnp.int32)
    zh = lax.axis_index("zh").astype(jnp.int32)
    last = (lax.axis_index(("zl", "x")) == NBLK - 1).astype(jnp.int32)
    k, j = merge_matrix.shape
    ut = deflate(kept_counts, deflation_order.reshape(1, k), merge_matrix.T)
    ut = lax.all_gather(ut, "core")
    ut_next = lax.ppermute(ut, ROUND, BACK)
    send, keep = divide(core.reshape(1), old_vectors, 8)
    got = lax.ppermute(send, "core", SWAP)
    early, late = multiply(jnp.stack([core, zh, last]), ut, ut_next, keep, got)
    early = lax.all_to_all(early, "y", 0, 0, tiled=True)
    early1 = lax.ppermute(early[:, j:].sum(axis=0), ROUND, AHEAD)
    early0 = early[:, :j].sum(axis=0)
    mixed = jnp.stack([early0, early1])
    across = lax.ppermute(mixed, "zh", SWAP)
    late, _ = lax.optimization_barrier((late, mixed))
    late = lax.all_to_all(late, "y", 0, 0, tiled=True)
    late1 = lax.ppermute(late[:, j:].sum(axis=0), ROUND, AHEAD)
    late0 = late[:, :j].sum(axis=0)
    return jnp.stack([late0, late1]) + across


def solution(mesh):
    split = Mesh(mesh.devices.reshape(SIZES), AXES)
    blk, col = ("zl", "x"), ("y", "zh", "core")
    return jax.shard_map(
        shards,
        mesh=split,
        in_specs=(P(col, blk), P(col, blk), P(col), P(col)),
        out_specs=P(None, None, AXES),
        check_vma=False,
    )
```

time: 147 us -> 75.7 us (0.51)
  the two profiles are of different devices: /device:TPU:8 before, /device:TPU:1 now
where the time goes in v2:
time: 75.7 us; the launch traced here: 75.3 us
  starting transfers between devices  31.8 us (42%)
  waiting for transfers between devices  23.4 us (31%)
  blocking collectives  13.8 us (18%)
  Pallas kernels  3.08 us (4%)
  local copies, waits for them, and re-layouts  1.61 us (2%)
  other arithmetic  0.83 us (1%)
    all_to_all x1, blocking collectives, shards(): early = lax.all_to_all(early, 'y', 0, 0, tiled=True)  12 us
    ppermute x1, waiting for transfers between devices, shards(): across = lax.ppermute(mixed, 'zh', SWAP)  11.5 us
    ppermute x1, waiting for transfers between devices, shards(): early1 = lax.ppermute(early[:, j:].sum(axis=0), ROUND, AHEAD)  10.2 us
    ppermute x1, starting transfers between devices, shards(): ut_next = lax.ppermute(ut, ROUND, BACK)  9.72 us
    ppermute x1, starting transfers between devices, shards(): got = lax.ppermute(send, 'core', SWAP)  8.75 us
    ppermute x1, starting transfers between devices, shards(): across = lax.ppermute(mixed, 'zh', SWAP)  6.05 us
    all_to_all x1, starting transfers between devices, shards(): late = lax.all_to_all(late, 'y', 0, 0, tiled=True)  3.48 us
    pallas_call x1, Pallas kernels, multiply(): pl.pallas_call(multiply_kernel, out_shape=(out, out), in_specs=[SMEM, VME...  2.41 us
  transfers between devices with their start and end apart: 6, of which 4 were waited for; matrix products, arithmetic and copies ran while one was open for 0% of the time, Pallas kernels for 0%

profile of v2, /device:TPU:1, one launch (start us, length us, event | category | flops | bytes accessed | tf_op | source)
XLA Modules:
  0.0 75.3 jit_solution(14203061077947187195)
XLA Ops:
  0.0 0.0 copy-start.2
  0.0 0.0 copy-start
  0.0 1.6 %copy-done = f32[64,8192]{1,0:T(8,128)S(1)} copy-done((f32[64,8192]{1,0:T(8,128)S(1)}, f32[64,8192]{1,0:T(8,128)}, u32[]{:S(2)}) %copy-start) | copy-done | bytes 2097176
  1.6 0.0 copy-start.1
  1.6 0.5 divide.1
  2.2 8.7 %collective-permute-start.1 = (f32[8,64,512]{2,1,0:T(8,128)S(1)}, f32[8,64,512]{2,1,0:T(8,128)S(1)}, u32[]{:S(2)}, u32[]{:S(2)}) collective-permute-start(f32[8,64,512]{2,1,0:T(8,128)S(1)} %get-tuple-element.11), channel_id=1, source_target_pairs={{0,1},{1,0},{2,3},{3,2},{4,5},{5,4},{6,7},{7,6},{8,9},{9,8},{10,11... | collective-permute-start | bytes 3145736 | tf_op jit(solution)/shard_map/ppermute | solution.py:129
  11.6 0.0 copy-done.2
  11.6 0.0 copy-done.1
  11.6 0.1 deflate.1
  11.7 1.8 %all-gather = f32[64,64]{1,0:T(8,128)S(1)} all-gather(f32[32,64]{1,0:T(8,128)S(1)} %deflate.1), channel_id=2, replica_groups=mesh['zl'=8,'x'=4,'y'=4,'zh'=2,'core'=2] {'core'}, dimensions={0}, use_global_device_ids=true | all-gather | bytes 24576 | tf_op jit(solution)/shard_map/all_gather | solution.py:126
  13.5 9.7 %collective-permute-start = (f32[2,32,64]{2,1,0:T(8,128)S(1)}, f32[2,32,64]{2,1,0:T(8,128)S(1)}, u32[]{:S(2)}, u32[]{:S(2)}) collective-permute-start(f32[2,32,64]{2,1,0:T(8,128)S(1)} %bitcast.10), channel_id=1, source_target_pairs={{0,496},{2,498},{16,0},{18,2},{32,16},{34,18},{48,32},{50,34},{64,... | collective-permute-start | bytes 49160 | tf_op jit(solution)/shard_map/ppermute | solution.py:127
  23.3 0.1 pad_add_fusion.where_ref
  23.4 0.9 %collective-permute-done.next_ref = f32[2,32,64]{2,1,0:T(8,128)S(1)} collective-permute-done((f32[2,32,64]{2,1,0:T(8,128)S(1)}, f32[2,32,64]{2,1,0:T(8,128)S(1)}, u32[]{:S(2)}, u32[]{:S(2)}) %collective-permute-start) | collective-permute-done | bytes 16416 | tf_op jit(solution)/shard_map/ppermute | solution.py:127
  24.3 0.0 collective-permute-done.1.got_ref
  24.3 2.4 %multiply.1 = (f32[4,64,512]{2,1,0:T(8,128)S(1)}, f32[4,64,512]{2,1,0:T(8,128)}) custom-call(s32[3]{0:T(128)S(1)} %pad_add_fusion.where_ref, f32[2,32,64]{2,1,0:T(8,128)S(1)} %bitcast.11, f32[2,32,64]{2,1,0:T(8,128)S(1)} %collective-permute-done.next_ref, f32[8,64,512]{2,1,0:T(8,128)S(1)} %get-tuple-element.10.keep_ref, ...), custom_call_target="tpu_custom_call" | custom-call | tf_op jit(solution)/shard_map/multiply/pallas_call | solution.py:95
  26.7 12.0 %all_to_all.10 = f32[4,64,512]{2,1,0:T(8,128)S(1)} all-to-all(f32[4,64,512]{2,1,0:T(8,128)S(1)} %get-tuple-element.13), channel_id=1, replica_groups=mesh['zl'=8,'x'=4,'y'=4,'zh'=2,'core'=2] {'y'}, dimensions={0} | all-to-all | bytes 1048576 | tf_op jit(solution)/shard_map/all_to_all | solution.py:131
  38.7 1.9 %collective-permute-start.2 = (f32[32,512]{1,0:T(8,128)S(1)}, f32[32,512]{1,0:T(8,128)S(1)}, u32[]{:S(2)}, u32[]{:S(2)}) collective-permute-start(f32[32,512]{1,0:T(8,128)S(1)} %get-tuple-element.18), channel_id=1, source_target_pairs={{0,16},{2,18},{16,32},{18,34},{32,48},{34,50},{48,64},{50,66},{64,... | collective-permute-start | bytes 196616 | tf_op jit(solution)/shard_map/ppermute | solution.py:132
  40.6 10.2 %collective-permute-done.2 = f32[32,512]{1,0:T(8,128)S(1)} collective-permute-done((f32[32,512]{1,0:T(8,128)S(1)}, f32[32,512]{1,0:T(8,128)S(1)}, u32[]{:S(2)}, u32[]{:S(2)}) %collective-permute-start.2) | collective-permute-done | bytes 65568 | tf_op jit(solution)/shard_map/ppermute | solution.py:132
  50.8 3.5 %all-to-all-start.1 = ((f32[4,64,512]{2,1,0:T(8,128)}), f32[4,64,512]{2,1,0:T(8,128)S(1)}, u32[]{:S(2)}, u32[]{:S(2)}) async-start(f32[4,64,512]{2,1,0:T(8,128)} %get-tuple-element.14), calls=%async_computation.1 | async-start | bytes 1048576 | tf_op jit(solution)/shard_map/all_to_all | solution.py:137
  54.3 6.1 %collective-permute-start.4 = (f32[2,32,512]{2,1,0:T(8,128)S(1)}, f32[2,32,512]{2,1,0:T(8,128)S(1)}, u32[]{:S(2)}, u32[]{:S(2)}) collective-permute-start(f32[2,32,512]{2,1,0:T(8,128)S(1)} %pad_maximum_fusion), channel_id=1, source_target_pairs={{0,2},{2,0},{1,3},{3,1},{4,6},{6,4},{5,7},{7,5},{8,10},{10,8},{9,1... | collective-permute-start | bytes 393224 | tf_op jit(solution)/shard_map/ppermute | solution.py:135
  60.4 0.8 %all-to-all-done.1 = f32[4,64,512]{2,1,0:T(8,128)S(1)} async-done(((f32[4,64,512]{2,1,0:T(8,128)}), f32[4,64,512]{2,1,0:T(8,128)S(1)}, u32[]{:S(2)}, u32[]{:S(2)}) %all-to-all-start.1) | async-done | bytes 524320 | tf_op jit(solution)/shard_map/all_to_all | solution.py:137
  61.3 1.9 %collective-permute-start.3 = (f32[32,512]{1,0:T(8,128)S(1)}, f32[32,512]{1,0:T(8,128)S(1)}, u32[]{:S(2)}, u32[]{:S(2)}) collective-permute-start(f32[32,512]{1,0:T(8,128)S(1)} %get-tuple-element.16), channel_id=1, source_target_pairs={{0,16},{2,18},{16,32},{18,34},{32,48},{34,50},{48,64},{50,66},{64,... | collective-permute-start | bytes 196616 | tf_op jit(solution)/shard_map/ppermute | solution.py:138
  63.2 11.5 %collective-permute-done.4 = f32[2,32,512]{2,1,0:T(8,128)S(1)} collective-permute-done((f32[2,32,512]{2,1,0:T(8,128)S(1)}, f32[2,32,512]{2,1,0:T(8,128)S(1)}, u32[]{:S(2)}, u32[]{:S(2)}) %collective-permute-start.4) | collective-permute-done | bytes 131104 | tf_op jit(solution)/shard_map/ppermute | solution.py:135
  74.7 0.0 collective-permute-done.3
  74.7 0.7 maximum_add_fusion
  (3 shorter events, 0.1 us)
Async XLA Ops:
  0.0 11.6 %copy-start.2 = (s32[64]{0:T(128)S(1)}, s32[64]{0:T(128)}, u32[]{:S(2)}) copy-start(s32[64]{0:T(128)} %param.6) | copy-start | bytes 772
  0.0 1.6 %copy-start = (f32[64,8192]{1,0:T(8,128)S(1)}, f32[64,8192]{1,0:T(8,128)}, u32[]{:S(2)}) copy-start(f32[64,8192]{1,0:T(8,128)} %q_ref.1) | copy-start | bytes 6291460
  1.6 10.0 %copy-start.1 = (f32[64,32]{0,1:T(8,128)S(1)}, f32[64,32]{0,1:T(8,128)}, u32[]{:S(2)}) copy-start(f32[64,32]{0,1:T(8,128)} %param.5) | copy-start | bytes 24580
  2.2 22.1 %collective-permute-start.1 = (f32[8,64,512]{2,1,0:T(8,128)S(1)}, f32[8,64,512]{2,1,0:T(8,128)S(1)}, u32[]{:S(2)}, u32[]{:S(2)}) collective-permute-start(f32[8,64,512]{2,1,0:T(8,128)S(1)} %get-tuple-element.11), channel_id=1, source_target_pairs={{0,1},{1,0},{2,3},{3,2},{4,5},{5,4},{6,7},{7,6},{8,9},{9,8},{10,11... | collective-permute-start | bytes 3145736 | tf_op jit(solution)/shard_map/ppermute | solution.py:129
  13.5 10.7 %collective-permute-start = (f32[2,32,64]{2,1,0:T(8,128)S(1)}, f32[2,32,64]{2,1,0:T(8,128)S(1)}, u32[]{:S(2)}, u32[]{:S(2)}) collective-permute-start(f32[2,32,64]{2,1,0:T(8,128)S(1)} %bitcast.10), channel_id=1, source_target_pairs={{0,496},{2,498},{16,0},{18,2},{32,16},{34,18},{48,32},{50,34},{64,... | collective-permute-start | bytes 49160 | tf_op jit(solution)/shard_map/ppermute | solution.py:127
  38.7 12.1 %collective-permute-start.2 = (f32[32,512]{1,0:T(8,128)S(1)}, f32[32,512]{1,0:T(8,128)S(1)}, u32[]{:S(2)}, u32[]{:S(2)}) collective-permute-start(f32[32,512]{1,0:T(8,128)S(1)} %get-tuple-element.18), channel_id=1, source_target_pairs={{0,16},{2,18},{16,32},{18,34},{32,48},{34,50},{48,64},{50,66},{64,... | collective-permute-start | bytes 196616 | tf_op jit(solution)/shard_map/ppermute | solution.py:132
  50.8 10.4 %all-to-all-start.1 = ((f32[4,64,512]{2,1,0:T(8,128)}), f32[4,64,512]{2,1,0:T(8,128)S(1)}, u32[]{:S(2)}, u32[]{:S(2)}) async-start(f32[4,64,512]{2,1,0:T(8,128)} %get-tuple-element.14), calls=%async_computation.1 | async-start | bytes 1048576 | tf_op jit(solution)/shard_map/all_to_all | solution.py:137
  54.3 20.3 %collective-permute-start.4 = (f32[2,32,512]{2,1,0:T(8,128)S(1)}, f32[2,32,512]{2,1,0:T(8,128)S(1)}, u32[]{:S(2)}, u32[]{:S(2)}) collective-permute-start(f32[2,32,512]{2,1,0:T(8,128)S(1)} %pad_maximum_fusion), channel_id=1, source_target_pairs={{0,2},{2,0},{1,3},{3,1},{4,6},{6,4},{5,7},{7,5},{8,10},{10,8},{9,1... | collective-permute-start | bytes 393224 | tf_op jit(solution)/shard_map/ppermute | solution.py:135
  61.3 13.4 %collective-permute-start.3 = (f32[32,512]{1,0:T(8,128)S(1)}, f32[32,512]{1,0:T(8,128)S(1)}, u32[]{:S(2)}, u32[]{:S(2)}) collective-permute-start(f32[32,512]{1,0:T(8,128)S(1)} %get-tuple-element.16), channel_id=1, source_target_pairs={{0,16},{2,18},{16,32},{18,34},{32,48},{34,50},{48,64},{50,66},{64,... | collective-permute-start | bytes 196616 | tf_op jit(solution)/shard_map/ppermute | solution.py:138

commit v3 on v2

v3 whole, which is shorter than its diff:
```python
import jax
import jax.numpy as jnp
from jax import lax
from jax.experimental import pallas as pl
from jax.experimental.pallas import tpu as pltpu
from jax.sharding import Mesh, PartitionSpec as P


AXES = ("zl", "x", "y", "zh", "core")
SIZES = (8, 4, 4, 2, 2)
NBLK = 32
LIMIT = pltpu.CompilerParams(vmem_limit_bytes=8 * 1024 * 1024)
SMEM = pl.BlockSpec(memory_space=pltpu.SMEM)
VMEM = pl.BlockSpec(memory_space=pltpu.VMEM)
ANY = pl.BlockSpec(memory_space=pl.ANY)


def in_hbm(value):
    return pltpu.with_memory_space_constraint(value, pltpu.HBM)


def divide_kernel(core_ref, q_ref, send_ref, keep_ref, sem):
    pieces, _, width = send_ref.shape
    copies = []
    for side, target in ((1 - core_ref[0], send_ref), (core_ref[0], keep_ref)):
        for g in range(pieces):
            start = pl.multiple_of((2 * g + side) * width, width)
            copies.append(
                pltpu.make_async_copy(q_ref.at[:, pl.ds(start, width)], target.at[g], sem.at[len(copies)])
            )
    for c in copies:
        c.start()
    for c in copies:
        c.wait()


def divide(core, q, pieces):
    half = pltpu.VMEM((pieces, q.shape[0], q.shape[1] // (2 * pieces)), jnp.float32)
    return pl.pallas_call(
        divide_kernel,
        out_shape=(half, half),
        in_specs=[SMEM, ANY],
        out_specs=(VMEM, VMEM),
        scratch_shapes=[pltpu.SemaphoreType.DMA((2 * pieces,))],
        compiler_params=LIMIT,
        name="divide",
    )(core, in_hbm(q))


def deflate_kernel(kept_ref, order_ref, here_ref, next_ref, out_ref):
    _, n = here_ref.shape
    rows = lax.broadcasted_iota(jnp.int32, (n, n), 0)
    place = lax.broadcasted_iota(jnp.int32, (n, n), 1)
    hit = (rows == order_ref[...]) & (place < kept_ref[0])
    out_ref[...] = lax.dot_general(
        jnp.concatenate([here_ref[...], next_ref[...]], axis=0),
        hit.astype(jnp.float32),
        (((1,), (0,)), ((), ())),
        precision=lax.Precision.HIGHEST,
        preferred_element_type=jnp.float32,
    )


def deflate(kept, order, here, following):
    j, n = here.shape
    return pl.pallas_call(
        deflate_kernel,
        out_shape=pltpu.VMEM((2 * j, n), jnp.float32),
        in_specs=[SMEM, VMEM, VMEM, VMEM],
        out_specs=VMEM,
        compiler_params=LIMIT,
        name="deflate",
    )(kept, order, here, following)


def split(value):
    high = value.astype(jnp.bfloat16)
    low = (value - high.astype(jnp.float32)).astype(jnp.bfloat16)
    return high, low


def left_operand(u):
    high, low = split(u)
    return jnp.concatenate(
        [jnp.concatenate([high, high], axis=1), jnp.concatenate([low, jnp.zeros_like(low)], axis=1)], axis=0
    )


def right_operand(keep, got):
    kh, kl = split(keep)
    gh, gl = split(got)
    return jnp.concatenate([kh, gh, kl, gl], axis=0)


def product(left, right):
    both = lax.dot_general(left, right, (((1,), (0,)), ((), ())), preferred_element_type=jnp.float32)
    rows = left.shape[0] // 2
    return both[:rows] + both[rows:]


def first_kernel(where_ref, ut_ref, keep_ref, got_ref, out_ref):
    core, zh = where_ref[0], where_ref[1]
    u = jnp.concatenate([ut_ref[core], ut_ref[1 - core]], axis=1)
    j = u.shape[0] // 2
    both, last = left_operand(u), left_operand(u[j:])
    for y in range(out_ref.shape[0]):
        far, near = 2 * y + 1 - zh, 2 * y + zh
        out_ref[y, : 2 * j] = product(both, right_operand(keep_ref[far], got_ref[far]))
        out_ref[y, 2 * j :] = product(last, right_operand(keep_ref[near], got_ref[near]))


def second_kernel(where_ref, ut_ref, keep_ref, got_ref, out_ref):
    core, zh = where_ref[0], where_ref[1]
    u = jnp.concatenate([ut_ref[core], ut_ref[1 - core]], axis=1)
    left = left_operand(u[: u.shape[0] // 2])
    for y in range(out_ref.shape[0]):
        near = 2 * y + zh
        out_ref[y] = product(left, right_operand(keep_ref[near], got_ref[near]))


def multiply(kernel, rows, where, ut, keep, got):
    pieces, _, width = keep.shape
    return pl.pallas_call(
        kernel,
        out_shape=pltpu.VMEM((pieces // 2, rows, width), jnp.float32),
        in_specs=[SMEM, VMEM, VMEM, VMEM],
        out_specs=VMEM,
        compiler_params=LIMIT,
    )(where, ut, keep, got)


def pairs_of(blocks, move):
    pairs = []
    for b in blocks:
        for zh in range(2):
            tb, tz = move(b, zh)
            pairs.append((b * 2 + zh, tb * 2 + tz))
    return pairs


LAST = NBLK - 1
BACK = pairs_of(range(NBLK), lambda b, zh: ((b - 1) % NBLK, zh))
AHEAD = pairs_of(range(LAST), lambda b, zh: (b + 1, zh))
WRAP_SAME = pairs_of([LAST], lambda b, zh: (0, zh))
WRAP_OTHER = pairs_of([LAST], lambda b, zh: (0, 1 - zh))
SWAP = [(0, 1), (1, 0)]
ROUND = ("zl", "x", "zh")


def over_y(value):
    return lax.all_to_all(value, "y", 0, 0, tiled=True)


def shards(old_vectors, merge_matrix, deflation_order, kept_counts):
    core = lax.axis_index("core").astype(jnp.int32)
    zh = lax.axis_index("zh").astype(jnp.int32)
    where = jnp.stack([core, zh])
    k, j = merge_matrix.shape
    merge_t = merge_matrix.T
    following = lax.ppermute(merge_t, ROUND, BACK)
    send, keep = divide(core.reshape(1), old_vectors, 8)
    got = lax.ppermute(send, "core", SWAP)
    ut = deflate(kept_counts, deflation_order.reshape(1, k), merge_t, following)
    ut = lax.all_gather(ut, "core")
    first = multiply(first_kernel, 3 * j, where, ut, keep, got)
    first = over_y(first)
    keep = lax.optimization_barrier((keep, first))[0]
    sum1 = first[:, j:].sum(axis=0)
    moved = lax.ppermute(sum1, ROUND, AHEAD)
    other = lax.ppermute(sum1[:j], ROUND, WRAP_OTHER)
    same = lax.ppermute(sum1[j:], ROUND, WRAP_SAME)
    sum0 = first[:, :j].sum(axis=0)
    across = lax.ppermute(jnp.concatenate([sum0, moved[:j]], axis=0), "zh", SWAP)
    second = multiply(second_kernel, j, where, ut, keep, got)
    second = over_y(second)
    second, moved, same, other, across = lax.optimization_barrier((second, moved, same, other, across))
    own = jnp.concatenate([second.sum(axis=0), moved[j:] + same + other], axis=0)
    return (own + across).reshape(2, j, -1)


def solution(mesh):
    split = Mesh(mesh.devices.reshape(SIZES), AXES)
    blk, col = ("zl", "x"), ("y", "zh", "core")
    return jax.shard_map(
        shards,
        mesh=split,
        in_specs=(P(col, blk), P(col, blk), P(col), P(col)),
        out_specs=P(None, None, AXES),
        check_vma=False,
    )
```

time: 75.7 us -> 72.8 us (0.962)
  the two profiles are of different devices: /device:TPU:1 before, /device:TPU:8 now
where the time goes in v3:
time: 72.8 us; the launch traced here: 72.4 us
  starting transfers between devices  34.2 us (47%)
  blocking collectives  17.7 us (24%)
  waiting for transfers between devices  14.3 us (20%)
  Pallas kernels  4.55 us (6%)
  other arithmetic  0.85 us (1%)
  between operations  0.78 us (1%)
    all_to_all x1, blocking collectives, over_y(): return lax.all_to_all(value, 'y', 0, 0, tiled=True)  15.9 us
    ppermute x1, starting transfers between devices, shards(): following = lax.ppermute(merge_t, ROUND, BACK)  15.4 us
    ppermute x1, waiting for transfers between devices, shards(): other = lax.ppermute(sum1[:j], ROUND, WRAP_OTHER)  9.09 us
    ppermute x1, starting transfers between devices, shards(): lax.ppermute(jnp.concatenate([sum0, moved[:j]], axis=0), 'zh', SWAP)  8.22 us
    all_to_all x1, starting transfers between devices, over_y(): return lax.all_to_all(value, 'y', 0, 0, tiled=True)  4.83 us
    ppermute x1, waiting for transfers between devices, shards(): same = lax.ppermute(sum1[j:], ROUND, WRAP_SAME)  4.49 us
    pallas_call x2, Pallas kernels, multiply(): pl.pallas_call(kernel, out_shape=pltpu.VMEM((pieces // 2, rows, width), j...  2.64 us
    ppermute x1, starting transfers between devices, shards(): got = lax.ppermute(send, 'core', SWAP)  1.92 us
  transfers between devices with their start and end apart: 7, of which 3 were waited for; matrix products, arithmetic and copies ran while one was open for 0% of the time, Pallas kernels for 2%

profile of v3, /device:TPU:8, one launch (start us, length us, event | category | flops | bytes accessed | tf_op | source)
XLA Modules:
  0.0 72.4 jit_solution(3649831007794237288)
XLA Ops:
  0.0 0.0 copy-start
  0.0 0.0 copy-start.1
  0.0 1.8 %divide.1 = (f32[8,64,512]{2,1,0:T(8,128)S(1)}, f32[8,64,512]{2,1,0:T(8,128)S(1)}) custom-call(s32[1]{0:T(128)} %bitcast.core_ref, f32[64,8192]{1,0:T(8,128)} %q_ref.1), custom_call_target="tpu_custom_call" | custom-call | tf_op jit(solution)/shard_map/divide/pallas_call | solution.py:39
  1.8 1.9 %collective-permute-start.1 = (f32[8,64,512]{2,1,0:T(8,128)S(1)}, f32[8,64,512]{2,1,0:T(8,128)S(1)}, u32[]{:S(2)}, u32[]{:S(2)}) collective-permute-start(f32[8,64,512]{2,1,0:T(8,128)S(1)} %get-tuple-element.14), channel_id=1, source_target_pairs={{0,1},{1,0},{2,3},{3,2},{4,5},{5,4},{6,7},{7,6},{8,9},{9,8},{10,11... | collective-permute-start | bytes 3145736 | tf_op jit(solution)/shard_map/ppermute | solution.py:162
  3.7 0.0 copy-done
  3.7 15.4 %collective-permute-start = (f32[32,64]{1,0:T(8,128)S(1)}, f32[32,64]{1,0:T(8,128)S(1)}, u32[]{:S(2)}, u32[]{:S(2)}) collective-permute-start(f32[32,64]{1,0:T(8,128)S(1)} %bitcast.8), channel_id=1, source_target_pairs={{0,496},{2,498},{16,0},{18,2},{32,16},{34,18},{48,32},{50,34},{64,... | collective-permute-start | bytes 24584 | tf_op jit(solution)/shard_map/ppermute | solution.py:160
  19.1 0.1 pad_add_fusion.where_ref
  19.8 0.7 collective-permute-done.next_ref
  20.5 0.0 copy-done.1
  20.5 0.1 deflate.1
  20.6 1.9 %all-gather = f32[128,64]{1,0:T(8,128)S(1)} all-gather(f32[64,64]{1,0:T(8,128)S(1)} %deflate.1), channel_id=2, replica_groups=mesh['zl'=8,'x'=4,'y'=4,'zh'=2,'core'=2] {'core'}, dimensions={0}, use_global_device_ids=true | all-gather | bytes 49152 | tf_op jit(solution)/shard_map/all_gather | solution.py:164
  22.5 0.0 collective-permute-done.1.got_ref
  22.5 1.1 %shard_map.46 = f32[4,96,512]{2,1,0:T(8,128)S(1)} custom-call(s32[2]{0:T(128)S(1)} %pad_add_fusion.where_ref, f32[2,64,64]{2,1,0:T(8,128)S(1)} %bitcast.6, f32[8,64,512]{2,1,0:T(8,128)S(1)} %get-tuple-element.15.keep_ref, f32[8,64,512]{2,1,0:T(8,128)S(1)} %collective-permute-done.1.got_ref), custom_call_target="tpu_custom_call" | custom-call | tf_op jit(solution)/shard_map/pallas_call | solution.py:123
  23.6 15.9 %all_to_all.10 = f32[4,96,512]{2,1,0:T(8,128)S(1)} all-to-all(f32[4,96,512]{2,1,0:T(8,128)S(1)} %shard_map.46), channel_id=1, replica_groups=mesh['zl'=8,'x'=4,'y'=4,'zh'=2,'core'=2] {'y'}, dimensions={0} | all-to-all | bytes 1572864 | tf_op jit(solution)/shard_map/all_to_all | solution.py:151
  39.5 1.3 %collective-permute-start.2 = (f32[64,512]{1,0:T(8,128)S(1)}, f32[64,512]{1,0:T(8,128)S(1)}, u32[]{:S(2)}, u32[]{:S(2)}) collective-permute-start(f32[64,512]{1,0:T(8,128)S(1)} %slice_reduce_fusion), channel_id=1, source_target_pairs={{0,16},{2,18},{16,32},{18,34},{32,48},{34,50},{48,64},{50,66},{64,... | collective-permute-start | bytes 393224 | tf_op jit(solution)/shard_map/ppermute | solution.py:169
  40.8 1.6 %shard_map.47 = f32[4,32,512]{2,1,0:T(8,128)} custom-call(s32[2]{0:T(128)S(1)} %pad_add_fusion.where_ref, f32[2,64,64]{2,1,0:T(8,128)S(1)} %bitcast.7, f32[8,64,512]{2,1,0:T(8,128)S(1)} %get-tuple-element.15.keep_ref, f32[8,64,512]{2,1,0:T(8,128)S(1)} %collective-permute-done.1.got_ref), custom_call_target="tpu_custom_call" | custom-call | tf_op jit(solution)/shard_map/pallas_call | solution.py:123
  42.3 4.8 %all-to-all-start.1 = ((f32[4,32,512]{2,1,0:T(8,128)}), f32[4,32,512]{2,1,0:T(8,128)S(1)}, u32[]{:S(2)}, u32[]{:S(2)}) async-start(f32[4,32,512]{2,1,0:T(8,128)} %shard_map.47), calls=%async_computation.1 | async-start | bytes 524288 | tf_op jit(solution)/shard_map/all_to_all | solution.py:151
  47.2 0.0 collective-permute-done.2
  47.2 8.2 %collective-permute-start.5 = (f32[64,512]{1,0:T(8,128)S(1)}, f32[64,512]{1,0:T(8,128)S(1)}, u32[]{:S(2)}, u32[]{:S(2)}) collective-permute-start(f32[64,512]{1,0:T(8,128)S(1)} %pad_maximum_fusion), channel_id=1, source_target_pairs={{0,2},{2,0},{1,3},{3,1},{4,6},{6,4},{5,7},{7,5},{8,10},{10,8},{9,1... | collective-permute-start | bytes 393224 | tf_op jit(solution)/shard_map/ppermute | solution.py:173
  55.5 1.3 %collective-permute-start.4 = (f32[32,512]{1,0:T(8,128)S(1)}, f32[32,512]{1,0:T(8,128)S(1)}, u32[]{:S(2)}, u32[]{:S(2)}) collective-permute-start(f32[32,512]{1,0:T(8,128)S(1)} %get-tuple-element.21), channel_id=1, source_target_pairs={{496,2},{498,0},{497,3},{499,1},{500,6},{502,4},{501,7},{503,5},{5... | collective-permute-start | bytes 196616 | tf_op jit(solution)/shard_map/ppermute | solution.py:170
  56.8 1.3 %collective-permute-start.3 = (f32[32,512]{1,0:T(8,128)S(1)}, f32[32,512]{1,0:T(8,128)S(1)}, u32[]{:S(2)}, u32[]{:S(2)}) collective-permute-start(f32[32,512]{1,0:T(8,128)S(1)} %get-tuple-element.22), channel_id=1, source_target_pairs={{496,0},{498,2},{497,1},{499,3},{500,4},{502,6},{501,5},{503,7},{5... | collective-permute-start | bytes 196616 | tf_op jit(solution)/shard_map/ppermute | solution.py:171
  58.1 9.1 %collective-permute-done.4 = f32[32,512]{1,0:T(8,128)S(1)} collective-permute-done((f32[32,512]{1,0:T(8,128)S(1)}, f32[32,512]{1,0:T(8,128)S(1)}, u32[]{:S(2)}, u32[]{:S(2)}) %collective-permute-start.4) | collective-permute-done | bytes 65568 | tf_op jit(solution)/shard_map/ppermute | solution.py:170
  67.2 4.5 %collective-permute-done.3 = f32[32,512]{1,0:T(8,128)S(1)} collective-permute-done((f32[32,512]{1,0:T(8,128)S(1)}, f32[32,512]{1,0:T(8,128)S(1)}, u32[]{:S(2)}, u32[]{:S(2)}) %collective-permute-start.3) | collective-permute-done | bytes 65568 | tf_op jit(solution)/shard_map/ppermute | solution.py:171
  71.7 0.0 all-to-all-done.1
  71.7 0.0 collective-permute-done.5
  71.7 0.7 maximum_add_fusion
  (7 shorter events, 0.1 us)
Async XLA Ops:
  0.0 3.7 %copy-start = (f32[64,32]{0,1:T(8,128)S(1)}, f32[64,32]{0,1:T(8,128)}, u32[]{:S(2)}) copy-start(f32[64,32]{0,1:T(8,128)} %param.5) | copy-start | bytes 24580
  0.0 20.5 %copy-start.1 = (s32[64]{0:T(128)S(1)}, s32[64]{0:T(128)}, u32[]{:S(2)}) copy-start(s32[64]{0:T(128)} %param.6) | copy-start | bytes 772
  1.8 20.7 %collective-permute-start.1 = (f32[8,64,512]{2,1,0:T(8,128)S(1)}, f32[8,64,512]{2,1,0:T(8,128)S(1)}, u32[]{:S(2)}, u32[]{:S(2)}) collective-permute-start(f32[8,64,512]{2,1,0:T(8,128)S(1)} %get-tuple-element.14), channel_id=1, source_target_pairs={{0,1},{1,0},{2,3},{3,2},{4,5},{5,4},{6,7},{7,6},{8,9},{9,8},{10,11... | collective-permute-start | bytes 3145736 | tf_op jit(solution)/shard_map/ppermute | solution.py:162
  3.7 16.8 %collective-permute-start = (f32[32,64]{1,0:T(8,128)S(1)}, f32[32,64]{1,0:T(8,128)S(1)}, u32[]{:S(2)}, u32[]{:S(2)}) collective-permute-start(f32[32,64]{1,0:T(8,128)S(1)} %bitcast.8), channel_id=1, source_target_pairs={{0,496},{2,498},{16,0},{18,2},{32,16},{34,18},{48,32},{50,34},{64,... | collective-permute-start | bytes 24584 | tf_op jit(solution)/shard_map/ppermute | solution.py:160
  39.5 7.7 %collective-permute-start.2 = (f32[64,512]{1,0:T(8,128)S(1)}, f32[64,512]{1,0:T(8,128)S(1)}, u32[]{:S(2)}, u32[]{:S(2)}) collective-permute-start(f32[64,512]{1,0:T(8,128)S(1)} %slice_reduce_fusion), channel_id=1, source_target_pairs={{0,16},{2,18},{16,32},{18,34},{32,48},{34,50},{48,64},{50,66},{64,... | collective-permute-start | bytes 393224 | tf_op jit(solution)/shard_map/ppermute | solution.py:169
  42.3 29.3 %all-to-all-start.1 = ((f32[4,32,512]{2,1,0:T(8,128)}), f32[4,32,512]{2,1,0:T(8,128)S(1)}, u32[]{:S(2)}, u32[]{:S(2)}) async-start(f32[4,32,512]{2,1,0:T(8,128)} %shard_map.47), calls=%async_computation.1 | async-start | bytes 524288 | tf_op jit(solution)/shard_map/all_to_all | solution.py:151
  47.2 24.4 %collective-permute-start.5 = (f32[64,512]{1,0:T(8,128)S(1)}, f32[64,512]{1,0:T(8,128)S(1)}, u32[]{:S(2)}, u32[]{:S(2)}) collective-permute-start(f32[64,512]{1,0:T(8,128)S(1)} %pad_maximum_fusion), channel_id=1, source_target_pairs={{0,2},{2,0},{1,3},{3,1},{4,6},{6,4},{5,7},{7,5},{8,10},{10,8},{9,1... | collective-permute-start | bytes 393224 | tf_op jit(solution)/shard_map/ppermute | solution.py:173
  55.5 11.7 %collective-permute-start.4 = (f32[32,512]{1,0:T(8,128)S(1)}, f32[32,512]{1,0:T(8,128)S(1)}, u32[]{:S(2)}, u32[]{:S(2)}) collective-permute-start(f32[32,512]{1,0:T(8,128)S(1)} %get-tuple-element.21), channel_id=1, source_target_pairs={{496,2},{498,0},{497,3},{499,1},{500,6},{502,4},{501,7},{503,5},{5... | collective-permute-start | bytes 196616 | tf_op jit(solution)/shard_map/ppermute | solution.py:170
  56.8 14.9 %collective-permute-start.3 = (f32[32,512]{1,0:T(8,128)S(1)}, f32[32,512]{1,0:T(8,128)S(1)}, u32[]{:S(2)}, u32[]{:S(2)}) collective-permute-start(f32[32,512]{1,0:T(8,128)S(1)} %get-tuple-element.22), channel_id=1, source_target_pairs={{496,0},{498,2},{497,1},{499,3},{500,4},{502,6},{501,5},{503,7},{5... | collective-permute-start | bytes 196616 | tf_op jit(solution)/shard_map/ppermute | solution.py:171

commit v4 on v3

--- a/solution.py
+++ b/solution.py
@@ -140,9 +140,10 @@
 
 LAST = NBLK - 1
 BACK = pairs_of(range(NBLK), lambda b, zh: ((b - 1) % NBLK, zh))
-AHEAD = pairs_of(range(LAST), lambda b, zh: (b + 1, zh))
-WRAP_SAME = pairs_of([LAST], lambda b, zh: (0, zh))
-WRAP_OTHER = pairs_of([LAST], lambda b, zh: (0, 1 - zh))
+AHEAD = pairs_of(range(1, LAST), lambda b, zh: (b + 1, zh))
+WRAP_SAME = pairs_of([LAST, 0], lambda b, zh: ((b + 1) % NBLK, zh))
+WRAP_OTHER = pairs_of([LAST], lambda b, zh: (0, 1 - zh)) + pairs_of([0], lambda b, zh: (1, 1 - zh))[1:]
+NEXT_OTHER = pairs_of([0], lambda b, zh: (1, 1 - zh))[:1]
 SWAP = [(0, 1), (1, 0)]
 ROUND = ("zl", "x", "zh")
 
@@ -171,10 +172,11 @@
     same = lax.ppermute(sum1[j:], ROUND, WRAP_SAME)
     sum0 = first[:, :j].sum(axis=0)
     across = lax.ppermute(jnp.concatenate([sum0, moved[:j]], axis=0), "zh", SWAP)
+    beyond = lax.ppermute(sum1[:j], ROUND, NEXT_OTHER)
     second = multiply(second_kernel, j, where, ut, keep, got)
     second = over_y(second)
-    second, moved, same, other, across = lax.optimization_barrier((second, moved, same, other, across))
-    own = jnp.concatenate([second.sum(axis=0), moved[j:] + same + other], axis=0)
+    second, moved, same, other, beyond, across = lax.optimization_barrier((second, moved, same, other, beyond, across))
+    own = jnp.concatenate([second.sum(axis=0), moved[j:] + same + other + beyond], axis=0)
     return (own + across).reshape(2, j, -1)
 
 

time: 72.8 us -> 72.8 us (level)
  the two profiles are of different devices: /device:TPU:8 before, /device:TPU:10 now
where the time goes in v4:
time: 72.8 us; the launch traced here: 72.4 us
  starting transfers between devices  29.6 us (41%)
  blocking collectives  19.7 us (27%)
  waiting for transfers between devices  16.9 us (23%)
  Pallas kernels  4.55 us (6%)
  other arithmetic  0.86 us (1%)
  between operations  0.78 us (1%)
    all_to_all x1, blocking collectives, over_y(): return lax.all_to_all(value, 'y', 0, 0, tiled=True)  17.9 us
    ppermute x1, starting transfers between devices, shards(): lax.ppermute(jnp.concatenate([sum0, moved[:j]], axis=0), 'zh', SWAP)  15.7 us
    ppermute x1, waiting for transfers between devices, shards(): other = lax.ppermute(sum1[:j], ROUND, WRAP_OTHER)  11.6 us
    all_to_all x1, starting transfers between devices, over_y(): return lax.all_to_all(value, 'y', 0, 0, tiled=True)  4.83 us
    ppermute x1, waiting for transfers between devices, shards(): same = lax.ppermute(sum1[j:], ROUND, WRAP_SAME)  2.89 us
    pallas_call x2, Pallas kernels, multiply(): pl.pallas_call(kernel, out_shape=pltpu.VMEM((pieces // 2, rows, width), j...  2.64 us
    ppermute x1, waiting for transfers between devices, shards(): following = lax.ppermute(merge_t, ROUND, BACK)  2.45 us
    ppermute x1, starting transfers between devices, shards(): following = lax.ppermute(merge_t, ROUND, BACK)  2.44 us
  transfers between devices with their start and end apart: 8, of which 3 were waited for; matrix products, arithmetic and copies ran while one was open for 0% of the time, Pallas kernels for 2%

profile of v4, /device:TPU:10, one launch (start us, length us, event | category | flops | bytes accessed | tf_op | source)
XLA Modules:
  0.0 72.4 jit_solution(10312677930455623960)
XLA Ops:
  0.0 0.0 copy-start
  0.0 0.0 copy-start.1
  0.0 1.8 %divide.1 = (f32[8,64,512]{2,1,0:T(8,128)S(1)}, f32[8,64,512]{2,1,0:T(8,128)S(1)}) custom-call(s32[1]{0:T(128)} %bitcast.core_ref, f32[64,8192]{1,0:T(8,128)} %q_ref.1), custom_call_target="tpu_custom_call" | custom-call | tf_op jit(solution)/shard_map/divide/pallas_call | solution.py:39
  1.8 1.9 %collective-permute-start.1 = (f32[8,64,512]{2,1,0:T(8,128)S(1)}, f32[8,64,512]{2,1,0:T(8,128)S(1)}, u32[]{:S(2)}, u32[]{:S(2)}) collective-permute-start(f32[8,64,512]{2,1,0:T(8,128)S(1)} %get-tuple-element.15), channel_id=1, source_target_pairs={{0,1},{1,0},{2,3},{3,2},{4,5},{5,4},{6,7},{7,6},{8,9},{9,8},{10,11... | collective-permute-start | bytes 3145736 | tf_op jit(solution)/shard_map/ppermute | solution.py:163
  3.7 0.0 copy-done
  3.7 2.4 %collective-permute-start = (f32[32,64]{1,0:T(8,128)S(1)}, f32[32,64]{1,0:T(8,128)S(1)}, u32[]{:S(2)}, u32[]{:S(2)}) collective-permute-start(f32[32,64]{1,0:T(8,128)S(1)} %bitcast.8), channel_id=1, source_target_pairs={{0,496},{2,498},{16,0},{18,2},{32,16},{34,18},{48,32},{50,34},{64,... | collective-permute-start | bytes 24584 | tf_op jit(solution)/shard_map/ppermute | solution.py:161
  6.2 0.1 pad_add_fusion.where_ref
  6.9 2.5 %collective-permute-done.next_ref = f32[32,64]{1,0:T(8,128)S(1)} collective-permute-done((f32[32,64]{1,0:T(8,128)S(1)}, f32[32,64]{1,0:T(8,128)S(1)}, u32[]{:S(2)}, u32[]{:S(2)}) %collective-permute-start) | collective-permute-done | bytes 8224 | tf_op jit(solution)/shard_map/ppermute | solution.py:161
  9.3 0.0 copy-done.1
  9.4 0.1 deflate.1
  9.5 1.9 %all-gather = f32[128,64]{1,0:T(8,128)S(1)} all-gather(f32[64,64]{1,0:T(8,128)S(1)} %deflate.1), channel_id=2, replica_groups=mesh['zl'=8,'x'=4,'y'=4,'zh'=2,'core'=2] {'core'}, dimensions={0}, use_global_device_ids=true | all-gather | bytes 49152 | tf_op jit(solution)/shard_map/all_gather | solution.py:165
  11.4 0.0 collective-permute-done.1.got_ref
  11.4 1.1 %shard_map.46 = f32[4,96,512]{2,1,0:T(8,128)S(1)} custom-call(s32[2]{0:T(128)S(1)} %pad_add_fusion.where_ref, f32[2,64,64]{2,1,0:T(8,128)S(1)} %bitcast.6, f32[8,64,512]{2,1,0:T(8,128)S(1)} %get-tuple-element.16.keep_ref, f32[8,64,512]{2,1,0:T(8,128)S(1)} %collective-permute-done.1.got_ref), custom_call_target="tpu_custom_call" | custom-call | tf_op jit(solution)/shard_map/pallas_call | solution.py:123
  12.4 17.9 %all_to_all.10 = f32[4,96,512]{2,1,0:T(8,128)S(1)} all-to-all(f32[4,96,512]{2,1,0:T(8,128)S(1)} %shard_map.46), channel_id=1, replica_groups=mesh['zl'=8,'x'=4,'y'=4,'zh'=2,'core'=2] {'y'}, dimensions={0} | all-to-all | bytes 1572864 | tf_op jit(solution)/shard_map/all_to_all | solution.py:152
  30.3 1.4 %collective-permute-start.2 = (f32[64,512]{1,0:T(8,128)S(1)}, f32[64,512]{1,0:T(8,128)S(1)}, u32[]{:S(2)}, u32[]{:S(2)}) collective-permute-start(f32[64,512]{1,0:T(8,128)S(1)} %slice_reduce_fusion), channel_id=1, source_target_pairs={{16,32},{18,34},{32,48},{34,50},{48,64},{50,66},{64,80},{66,82},{8... | collective-permute-start | bytes 393224 | tf_op jit(solution)/shard_map/ppermute | solution.py:170
  31.7 1.6 %shard_map.47 = f32[4,32,512]{2,1,0:T(8,128)} custom-call(s32[2]{0:T(128)S(1)} %pad_add_fusion.where_ref, f32[2,64,64]{2,1,0:T(8,128)S(1)} %bitcast.7, f32[8,64,512]{2,1,0:T(8,128)S(1)} %get-tuple-element.16.keep_ref, f32[8,64,512]{2,1,0:T(8,128)S(1)} %collective-permute-done.1.got_ref), custom_call_target="tpu_custom_call" | custom-call | tf_op jit(solution)/shard_map/pallas_call | solution.py:123
  33.3 4.8 %all-to-all-start.1 = ((f32[4,32,512]{2,1,0:T(8,128)}), f32[4,32,512]{2,1,0:T(8,128)S(1)}, u32[]{:S(2)}, u32[]{:S(2)}) async-start(f32[4,32,512]{2,1,0:T(8,128)} %shard_map.47), calls=%async_computation.1 | async-start | bytes 524288 | tf_op jit(solution)/shard_map/all_to_all | solution.py:152
  38.2 0.0 collective-permute-done.2
  38.2 15.7 %collective-permute-start.6 = (f32[64,512]{1,0:T(8,128)S(1)}, f32[64,512]{1,0:T(8,128)S(1)}, u32[]{:S(2)}, u32[]{:S(2)}) collective-permute-start(f32[64,512]{1,0:T(8,128)S(1)} %pad_maximum_fusion), channel_id=1, source_target_pairs={{0,2},{2,0},{1,3},{3,1},{4,6},{6,4},{5,7},{7,5},{8,10},{10,8},{9,1... | collective-permute-start | bytes 393224 | tf_op jit(solution)/shard_map/ppermute | solution.py:174
  54.0 1.3 %collective-permute-start.3 = (f32[32,512]{1,0:T(8,128)S(1)}, f32[32,512]{1,0:T(8,128)S(1)}, u32[]{:S(2)}, u32[]{:S(2)}) collective-permute-start(f32[32,512]{1,0:T(8,128)S(1)} %get-tuple-element.24), channel_id=1, source_target_pairs={{496,0},{498,2},{0,16},{2,18},{497,1},{499,3},{1,17},{3,19},{500,4... | collective-permute-start | bytes 196616 | tf_op jit(solution)/shard_map/ppermute | solution.py:172
  55.2 0.7 collective-permute-start.5
  55.9 1.3 %collective-permute-start.4 = (f32[32,512]{1,0:T(8,128)S(1)}, f32[32,512]{1,0:T(8,128)S(1)}, u32[]{:S(2)}, u32[]{:S(2)}) collective-permute-start(f32[32,512]{1,0:T(8,128)S(1)} %get-tuple-element.23), channel_id=1, source_target_pairs={{496,2},{498,0},{2,16},{497,3},{499,1},{3,17},{500,6},{502,4},{6,2... | collective-permute-start | bytes 196616 | tf_op jit(solution)/shard_map/ppermute | solution.py:171
  57.2 2.9 %collective-permute-done.3 = f32[32,512]{1,0:T(8,128)S(1)} collective-permute-done((f32[32,512]{1,0:T(8,128)S(1)}, f32[32,512]{1,0:T(8,128)S(1)}, u32[]{:S(2)}, u32[]{:S(2)}) %collective-permute-start.3) | collective-permute-done | bytes 65568 | tf_op jit(solution)/shard_map/ppermute | solution.py:172
  60.1 0.0 collective-permute-done.5
  60.1 11.6 %collective-permute-done.4 = f32[32,512]{1,0:T(8,128)S(1)} collective-permute-done((f32[32,512]{1,0:T(8,128)S(1)}, f32[32,512]{1,0:T(8,128)S(1)}, u32[]{:S(2)}, u32[]{:S(2)}) %collective-permute-start.4) | collective-permute-done | bytes 65568 | tf_op jit(solution)/shard_map/ppermute | solution.py:171
  71.7 0.0 all-to-all-done.1
  71.7 0.0 collective-permute-done.6
  71.8 0.7 maximum_add_fusion
  (7 shorter events, 0.1 us)
Async XLA Ops:
  0.0 3.7 %copy-start = (f32[64,32]{0,1:T(8,128)S(1)}, f32[64,32]{0,1:T(8,128)}, u32[]{:S(2)}) copy-start(f32[64,32]{0,1:T(8,128)} %param.5) | copy-start | bytes 24580
  0.0 9.3 %copy-start.1 = (s32[64]{0:T(128)S(1)}, s32[64]{0:T(128)}, u32[]{:S(2)}) copy-start(s32[64]{0:T(128)} %param.6) | copy-start | bytes 772
  1.8 9.6 %collective-permute-start.1 = (f32[8,64,512]{2,1,0:T(8,128)S(1)}, f32[8,64,512]{2,1,0:T(8,128)S(1)}, u32[]{:S(2)}, u32[]{:S(2)}) collective-permute-start(f32[8,64,512]{2,1,0:T(8,128)S(1)} %get-tuple-element.15), channel_id=1, source_target_pairs={{0,1},{1,0},{2,3},{3,2},{4,5},{5,4},{6,7},{7,6},{8,9},{9,8},{10,11... | collective-permute-start | bytes 3145736 | tf_op jit(solution)/shard_map/ppermute | solution.py:163
  3.7 5.6 %collective-permute-start = (f32[32,64]{1,0:T(8,128)S(1)}, f32[32,64]{1,0:T(8,128)S(1)}, u32[]{:S(2)}, u32[]{:S(2)}) collective-permute-start(f32[32,64]{1,0:T(8,128)S(1)} %bitcast.8), channel_id=1, source_target_pairs={{0,496},{2,498},{16,0},{18,2},{32,16},{34,18},{48,32},{50,34},{64,... | collective-permute-start | bytes 24584 | tf_op jit(solution)/shard_map/ppermute | solution.py:161
  30.3 7.8 %collective-permute-start.2 = (f32[64,512]{1,0:T(8,128)S(1)}, f32[64,512]{1,0:T(8,128)S(1)}, u32[]{:S(2)}, u32[]{:S(2)}) collective-permute-start(f32[64,512]{1,0:T(8,128)S(1)} %slice_reduce_fusion), channel_id=1, source_target_pairs={{16,32},{18,34},{32,48},{34,50},{48,64},{50,66},{64,80},{66,82},{8... | collective-permute-start | bytes 393224 | tf_op jit(solution)/shard_map/ppermute | solution.py:170
  33.3 38.4 %all-to-all-start.1 = ((f32[4,32,512]{2,1,0:T(8,128)}), f32[4,32,512]{2,1,0:T(8,128)S(1)}, u32[]{:S(2)}, u32[]{:S(2)}) async-start(f32[4,32,512]{2,1,0:T(8,128)} %shard_map.47), calls=%async_computation.1 | async-start | bytes 524288 | tf_op jit(solution)/shard_map/all_to_all | solution.py:152
  38.2 33.5 %collective-permute-start.6 = (f32[64,512]{1,0:T(8,128)S(1)}, f32[64,512]{1,0:T(8,128)S(1)}, u32[]{:S(2)}, u32[]{:S(2)}) collective-permute-start(f32[64,512]{1,0:T(8,128)S(1)} %pad_maximum_fusion), channel_id=1, source_target_pairs={{0,2},{2,0},{1,3},{3,1},{4,6},{6,4},{5,7},{7,5},{8,10},{10,8},{9,1... | collective-permute-start | bytes 393224 | tf_op jit(solution)/shard_map/ppermute | solution.py:174
  54.0 6.2 %collective-permute-start.3 = (f32[32,512]{1,0:T(8,128)S(1)}, f32[32,512]{1,0:T(8,128)S(1)}, u32[]{:S(2)}, u32[]{:S(2)}) collective-permute-start(f32[32,512]{1,0:T(8,128)S(1)} %get-tuple-element.24), channel_id=1, source_target_pairs={{496,0},{498,2},{0,16},{2,18},{497,1},{499,3},{1,17},{3,19},{500,4... | collective-permute-start | bytes 196616 | tf_op jit(solution)/shard_map/ppermute | solution.py:172
  55.2 4.9 %collective-permute-start.5 = (f32[32,512]{1,0:T(8,128)S(1)}, f32[32,512]{1,0:T(8,128)S(1)}, u32[]{:S(2)}, u32[]{:S(2)}) collective-permute-start(f32[32,512]{1,0:T(8,128)S(1)} %get-tuple-element.23), channel_id=1, source_target_pairs={{0,18},{1,19},{4,22},{5,23},{8,26},{9,27},{12,30},{13,31}} | collective-permute-start | bytes 196616 | tf_op jit(solution)/shard_map/ppermute | solution.py:175
  55.9 15.8 %collective-permute-start.4 = (f32[32,512]{1,0:T(8,128)S(1)}, f32[32,512]{1,0:T(8,128)S(1)}, u32[]{:S(2)}, u32[]{:S(2)}) collective-permute-start(f32[32,512]{1,0:T(8,128)S(1)} %get-tuple-element.23), channel_id=1, source_target_pairs={{496,2},{498,0},{2,16},{497,3},{499,1},{3,17},{500,6},{502,4},{6,2... | collective-permute-start | bytes 196616 | tf_op jit(solution)/shard_map/ppermute | solution.py:171

commit v5 on v4

--- a/solution.py
+++ b/solution.py
@@ -127,6 +127,23 @@
         out_specs=VMEM,
         compiler_params=LIMIT,
     )(where, ut, keep, got)
+
+
+def join_kernel(top_ref, moved_ref, out_ref):
+    j = top_ref.shape[0]
+    out_ref[:j] = top_ref[...]
+    out_ref[j:] = moved_ref[:j]
+
+
+def join(top, moved):
+    return pl.pallas_call(
+        join_kernel,
+        out_shape=pltpu.VMEM(moved.shape, jnp.float32),
+        in_specs=[VMEM, VMEM],
+        out_specs=VMEM,
+        compiler_params=LIMIT,
+        name="join",
+    )(top, moved)
 
 
 def pairs_of(blocks, move):
@@ -171,11 +188,13 @@
     other = lax.ppermute(sum1[:j], ROUND, WRAP_OTHER)
     same = lax.ppermute(sum1[j:], ROUND, WRAP_SAME)
     sum0 = first[:, :j].sum(axis=0)
-    across = lax.ppermute(jnp.concatenate([sum0, moved[:j]], axis=0), "zh", SWAP)
+    across = lax.ppermute(join(sum0, moved), "zh", SWAP)
     beyond = lax.ppermute(sum1[:j], ROUND, NEXT_OTHER)
     second = multiply(second_kernel, j, where, ut, keep, got)
     second = over_y(second)
-    second, moved, same, other, beyond, across = lax.optimization_barrier((second, moved, same, other, beyond, across))
+    second, moved, same, other, beyond, across = lax.optimization_barrier(
+        (second, moved, same, other, beyond, across)
+    )
     own = jnp.concatenate([second.sum(axis=0), moved[j:] + same + other + beyond], axis=0)
     return (own + across).reshape(2, j, -1)
 

time: 72.8 us -> 72.8 us (level)
  no operation moved by 1% of the time
where the time goes in v5:
time: 72.8 us; the launch traced here: 72.4 us
  starting transfers between devices  29.6 us (41%)
  blocking collectives  19.7 us (27%)
  waiting for transfers between devices  16.9 us (23%)
  Pallas kernels  4.56 us (6%)
  other arithmetic  0.85 us (1%)
  between operations  0.78 us (1%)
    all_to_all x1, blocking collectives, over_y(): return lax.all_to_all(value, 'y', 0, 0, tiled=True)  17.9 us
    ppermute x1, starting transfers between devices, shards(): across = lax.ppermute(join(sum0, moved), 'zh', SWAP)  15.7 us
    ppermute x1, waiting for transfers between devices, shards(): other = lax.ppermute(sum1[:j], ROUND, WRAP_OTHER)  11.6 us
    all_to_all x1, starting transfers between devices, over_y(): return lax.all_to_all(value, 'y', 0, 0, tiled=True)  4.83 us
    ppermute x1, waiting for transfers between devices, shards(): same = lax.ppermute(sum1[j:], ROUND, WRAP_SAME)  2.89 us
    pallas_call x2, Pallas kernels, multiply(): pl.pallas_call(kernel, out_shape=pltpu.VMEM((pieces // 2, rows, width), j...  2.64 us
    ppermute x1, waiting for transfers between devices, shards(): following = lax.ppermute(merge_t, ROUND, BACK)  2.45 us
    ppermute x1, starting transfers between devices, shards(): following = lax.ppermute(merge_t, ROUND, BACK)  2.44 us
  transfers between devices with their start and end apart: 8, of which 3 were waited for; matrix products, arithmetic and copies ran while one was open for 0% of the time, Pallas kernels for 2%

profile of v5, /device:TPU:10, one launch (start us, length us, event | category | flops | bytes accessed | tf_op | source)
XLA Modules:
  0.0 72.4 jit_solution(11738583174601362270)
XLA Ops:
  0.0 0.0 copy-start
  0.0 0.0 copy-start.1
  0.0 1.8 %divide.1 = (f32[8,64,512]{2,1,0:T(8,128)S(1)}, f32[8,64,512]{2,1,0:T(8,128)S(1)}) custom-call(s32[1]{0:T(128)} %bitcast.core_ref, f32[64,8192]{1,0:T(8,128)} %q_ref.1), custom_call_target="tpu_custom_call" | custom-call | tf_op jit(solution)/shard_map/divide/pallas_call | solution.py:39
  1.8 1.9 %collective-permute-start.1 = (f32[8,64,512]{2,1,0:T(8,128)S(1)}, f32[8,64,512]{2,1,0:T(8,128)S(1)}, u32[]{:S(2)}, u32[]{:S(2)}) collective-permute-start(f32[8,64,512]{2,1,0:T(8,128)S(1)} %get-tuple-element.15), channel_id=1, source_target_pairs={{0,1},{1,0},{2,3},{3,2},{4,5},{5,4},{6,7},{7,6},{8,9},{9,8},{10,11... | collective-permute-start | bytes 3145736 | tf_op jit(solution)/shard_map/ppermute | solution.py:180
  3.7 0.0 copy-done
  3.7 2.4 %collective-permute-start = (f32[32,64]{1,0:T(8,128)S(1)}, f32[32,64]{1,0:T(8,128)S(1)}, u32[]{:S(2)}, u32[]{:S(2)}) collective-permute-start(f32[32,64]{1,0:T(8,128)S(1)} %bitcast.8), channel_id=1, source_target_pairs={{0,496},{2,498},{16,0},{18,2},{32,16},{34,18},{48,32},{50,34},{64,... | collective-permute-start | bytes 24584 | tf_op jit(solution)/shard_map/ppermute | solution.py:178
  6.2 0.1 pad_add_fusion.where_ref
  6.9 2.5 %collective-permute-done.next_ref = f32[32,64]{1,0:T(8,128)S(1)} collective-permute-done((f32[32,64]{1,0:T(8,128)S(1)}, f32[32,64]{1,0:T(8,128)S(1)}, u32[]{:S(2)}, u32[]{:S(2)}) %collective-permute-start) | collective-permute-done | bytes 8224 | tf_op jit(solution)/shard_map/ppermute | solution.py:178
  9.3 0.0 copy-done.1
  9.4 0.1 deflate.1
  9.5 1.9 %all-gather = f32[128,64]{1,0:T(8,128)S(1)} all-gather(f32[64,64]{1,0:T(8,128)S(1)} %deflate.1), channel_id=2, replica_groups=mesh['zl'=8,'x'=4,'y'=4,'zh'=2,'core'=2] {'core'}, dimensions={0}, use_global_device_ids=true | all-gather | bytes 49152 | tf_op jit(solution)/shard_map/all_gather | solution.py:182
  11.4 0.0 collective-permute-done.1.got_ref
  11.4 1.1 %shard_map.46 = f32[4,96,512]{2,1,0:T(8,128)S(1)} custom-call(s32[2]{0:T(128)S(1)} %pad_add_fusion.where_ref, f32[2,64,64]{2,1,0:T(8,128)S(1)} %bitcast.6, f32[8,64,512]{2,1,0:T(8,128)S(1)} %get-tuple-element.16.keep_ref, f32[8,64,512]{2,1,0:T(8,128)S(1)} %collective-permute-done.1.got_ref), custom_call_target="tpu_custom_call" | custom-call | tf_op jit(solution)/shard_map/pallas_call | solution.py:123
  12.4 17.9 %all_to_all.10 = f32[4,96,512]{2,1,0:T(8,128)S(1)} all-to-all(f32[4,96,512]{2,1,0:T(8,128)S(1)} %shard_map.46), channel_id=1, replica_groups=mesh['zl'=8,'x'=4,'y'=4,'zh'=2,'core'=2] {'y'}, dimensions={0} | all-to-all | bytes 1572864 | tf_op jit(solution)/shard_map/all_to_all | solution.py:169
  30.3 1.4 %collective-permute-start.2 = (f32[64,512]{1,0:T(8,128)S(1)}, f32[64,512]{1,0:T(8,128)S(1)}, u32[]{:S(2)}, u32[]{:S(2)}) collective-permute-start(f32[64,512]{1,0:T(8,128)S(1)} %slice_reduce_fusion), channel_id=1, source_target_pairs={{16,32},{18,34},{32,48},{34,50},{48,64},{50,66},{64,80},{66,82},{8... | collective-permute-start | bytes 393224 | tf_op jit(solution)/shard_map/ppermute | solution.py:187
  31.7 1.6 %shard_map.47 = f32[4,32,512]{2,1,0:T(8,128)} custom-call(s32[2]{0:T(128)S(1)} %pad_add_fusion.where_ref, f32[2,64,64]{2,1,0:T(8,128)S(1)} %bitcast.7, f32[8,64,512]{2,1,0:T(8,128)S(1)} %get-tuple-element.16.keep_ref, f32[8,64,512]{2,1,0:T(8,128)S(1)} %collective-permute-done.1.got_ref), custom_call_target="tpu_custom_call" | custom-call | tf_op jit(solution)/shard_map/pallas_call | solution.py:123
  33.3 4.8 %all-to-all-start.1 = ((f32[4,32,512]{2,1,0:T(8,128)}), f32[4,32,512]{2,1,0:T(8,128)S(1)}, u32[]{:S(2)}, u32[]{:S(2)}) async-start(f32[4,32,512]{2,1,0:T(8,128)} %shard_map.47), calls=%async_computation.1 | async-start | bytes 524288 | tf_op jit(solution)/shard_map/all_to_all | solution.py:169
  38.2 0.0 collective-permute-done.2.moved_ref
  38.2 15.7 %collective-permute-start.6 = (f32[64,512]{1,0:T(8,128)S(1)}, f32[64,512]{1,0:T(8,128)S(1)}, u32[]{:S(2)}, u32[]{:S(2)}) collective-permute-start(f32[64,512]{1,0:T(8,128)S(1)} %join.1), channel_id=1, source_target_pairs={{0,2},{2,0},{1,3},{3,1},{4,6},{6,4},{5,7},{7,5},{8,10},{10,8},{9,1... | collective-permute-start | bytes 393224 | tf_op jit(solution)/shard_map/ppermute | solution.py:191
  53.9 1.3 %collective-permute-start.3 = (f32[32,512]{1,0:T(8,128)S(1)}, f32[32,512]{1,0:T(8,128)S(1)}, u32[]{:S(2)}, u32[]{:S(2)}) collective-permute-start(f32[32,512]{1,0:T(8,128)S(1)} %get-tuple-element.24), channel_id=1, source_target_pairs={{496,0},{498,2},{0,16},{2,18},{497,1},{499,3},{1,17},{3,19},{500,4... | collective-permute-start | bytes 196616 | tf_op jit(solution)/shard_map/ppermute | solution.py:189
  55.2 0.7 collective-permute-start.5
  55.9 1.3 %collective-permute-start.4 = (f32[32,512]{1,0:T(8,128)S(1)}, f32[32,512]{1,0:T(8,128)S(1)}, u32[]{:S(2)}, u32[]{:S(2)}) collective-permute-start(f32[32,512]{1,0:T(8,128)S(1)} %get-tuple-element.23), channel_id=1, source_target_pairs={{496,2},{498,0},{2,16},{497,3},{499,1},{3,17},{500,6},{502,4},{6,2... | collective-permute-start | bytes 196616 | tf_op jit(solution)/shard_map/ppermute | solution.py:188
  57.2 2.9 %collective-permute-done.3 = f32[32,512]{1,0:T(8,128)S(1)} collective-permute-done((f32[32,512]{1,0:T(8,128)S(1)}, f32[32,512]{1,0:T(8,128)S(1)}, u32[]{:S(2)}, u32[]{:S(2)}) %collective-permute-start.3) | collective-permute-done | bytes 65568 | tf_op jit(solution)/shard_map/ppermute | solution.py:189
  60.1 0.0 collective-permute-done.5
  60.1 11.6 %collective-permute-done.4 = f32[32,512]{1,0:T(8,128)S(1)} collective-permute-done((f32[32,512]{1,0:T(8,128)S(1)}, f32[32,512]{1,0:T(8,128)S(1)}, u32[]{:S(2)}, u32[]{:S(2)}) %collective-permute-start.4) | collective-permute-done | bytes 65568 | tf_op jit(solution)/shard_map/ppermute | solution.py:188
  71.7 0.0 all-to-all-done.1
  71.7 0.0 collective-permute-done.6
  71.7 0.7 maximum_add_fusion
  (6 shorter events, 0.1 us)
Async XLA Ops:
  0.0 3.7 %copy-start = (f32[64,32]{0,1:T(8,128)S(1)}, f32[64,32]{0,1:T(8,128)}, u32[]{:S(2)}) copy-start(f32[64,32]{0,1:T(8,128)} %param.5) | copy-start | bytes 24580
  0.0 9.3 %copy-start.1 = (s32[64]{0:T(128)S(1)}, s32[64]{0:T(128)}, u32[]{:S(2)}) copy-start(s32[64]{0:T(128)} %param.6) | copy-start | bytes 772
  1.8 9.6 %collective-permute-start.1 = (f32[8,64,512]{2,1,0:T(8,128)S(1)}, f32[8,64,512]{2,1,0:T(8,128)S(1)}, u32[]{:S(2)}, u32[]{:S(2)}) collective-permute-start(f32[8,64,512]{2,1,0:T(8,128)S(1)} %get-tuple-element.15), channel_id=1, source_target_pairs={{0,1},{1,0},{2,3},{3,2},{4,5},{5,4},{6,7},{7,6},{8,9},{9,8},{10,11... | collective-permute-start | bytes 3145736 | tf_op jit(solution)/shard_map/ppermute | solution.py:180
  3.7 5.6 %collective-permute-start = (f32[32,64]{1,0:T(8,128)S(1)}, f32[32,64]{1,0:T(8,128)S(1)}, u32[]{:S(2)}, u32[]{:S(2)}) collective-permute-start(f32[32,64]{1,0:T(8,128)S(1)} %bitcast.8), channel_id=1, source_target_pairs={{0,496},{2,498},{16,0},{18,2},{32,16},{34,18},{48,32},{50,34},{64,... | collective-permute-start | bytes 24584 | tf_op jit(solution)/shard_map/ppermute | solution.py:178
  30.3 7.8 %collective-permute-start.2 = (f32[64,512]{1,0:T(8,128)S(1)}, f32[64,512]{1,0:T(8,128)S(1)}, u32[]{:S(2)}, u32[]{:S(2)}) collective-permute-start(f32[64,512]{1,0:T(8,128)S(1)} %slice_reduce_fusion), channel_id=1, source_target_pairs={{16,32},{18,34},{32,48},{34,50},{48,64},{50,66},{64,80},{66,82},{8... | collective-permute-start | bytes 393224 | tf_op jit(solution)/shard_map/ppermute | solution.py:187
  33.3 38.4 %all-to-all-start.1 = ((f32[4,32,512]{2,1,0:T(8,128)}), f32[4,32,512]{2,1,0:T(8,128)S(1)}, u32[]{:S(2)}, u32[]{:S(2)}) async-start(f32[4,32,512]{2,1,0:T(8,128)} %shard_map.47), calls=%async_computation.1 | async-start | bytes 524288 | tf_op jit(solution)/shard_map/all_to_all | solution.py:169
  38.2 33.5 %collective-permute-start.6 = (f32[64,512]{1,0:T(8,128)S(1)}, f32[64,512]{1,0:T(8,128)S(1)}, u32[]{:S(2)}, u32[]{:S(2)}) collective-permute-start(f32[64,512]{1,0:T(8,128)S(1)} %join.1), channel_id=1, source_target_pairs={{0,2},{2,0},{1,3},{3,1},{4,6},{6,4},{5,7},{7,5},{8,10},{10,8},{9,1... | collective-permute-start | bytes 393224 | tf_op jit(solution)/shard_map/ppermute | solution.py:191
  53.9 6.2 %collective-permute-start.3 = (f32[32,512]{1,0:T(8,128)S(1)}, f32[32,512]{1,0:T(8,128)S(1)}, u32[]{:S(2)}, u32[]{:S(2)}) collective-permute-start(f32[32,512]{1,0:T(8,128)S(1)} %get-tuple-element.24), channel_id=1, source_target_pairs={{496,0},{498,2},{0,16},{2,18},{497,1},{499,3},{1,17},{3,19},{500,4... | collective-permute-start | bytes 196616 | tf_op jit(solution)/shard_map/ppermute | solution.py:189
  55.2 4.9 %collective-permute-start.5 = (f32[32,512]{1,0:T(8,128)S(1)}, f32[32,512]{1,0:T(8,128)S(1)}, u32[]{:S(2)}, u32[]{:S(2)}) collective-permute-start(f32[32,512]{1,0:T(8,128)S(1)} %get-tuple-element.23), channel_id=1, source_target_pairs={{0,18},{1,19},{4,22},{5,23},{8,26},{9,27},{12,30},{13,31}} | collective-permute-start | bytes 196616 | tf_op jit(solution)/shard_map/ppermute | solution.py:192
  55.9 15.8 %collective-permute-start.4 = (f32[32,512]{1,0:T(8,128)S(1)}, f32[32,512]{1,0:T(8,128)S(1)}, u32[]{:S(2)}, u32[]{:S(2)}) collective-permute-start(f32[32,512]{1,0:T(8,128)S(1)} %get-tuple-element.23), channel_id=1, source_target_pairs={{496,2},{498,0},{2,16},{497,3},{499,1},{3,17},{500,6},{502,4},{6,2... | collective-permute-start | bytes 196616 | tf_op jit(solution)/shard_map/ppermute | solution.py:188
